TPU v7x, 32 devices: a 4x4x1 block of a 4x4x8 slice. The times are simulated.
32 devices in a mesh: dp: 1 (over z), ep: 32 (over y, x, core).
Axes of the slice: x: 4, y: 4, z: 1, core: 2. Of those that a mesh axis runs over, the one named last changes fastest.
The devices are a block of a 4x4x8 slice.
Arguments:
- tokens: bfloat16 [8192, 1536], P(('dp', 'ep'))
- expert_ids: int32 [8192, 6], P(('dp', 'ep'))
- gate_vals: float32 [8192, 6], P(('dp', 'ep'))
- slots: int32 [8192, 6], P(('dp', 'ep'))
- shared_w1: bfloat16 [1536, 1024], replicated
- shared_w3: bfloat16 [1536, 1024], replicated
- shared_w2: bfloat16 [1024, 1536], replicated
- shared_gate: bfloat16 [1536], replicated
- expert_w1: bfloat16 [64, 1536, 512], P('ep')
- expert_w3: bfloat16 [64, 1536, 512], P('ep')
- expert_w2: bfloat16 [64, 512, 1536], P('ep')
Outputs:
- output: bfloat16 [8192, 1536], P(('dp', 'ep'))
All inputs are finite; a program needn't handle non-finite values.
Results may differ from a plain program's by a relative error of at most 0.00516558.
Values are sent between devices in bfloat16 or wider.
A program may use at most 768 MiB of HBM per device.

v0:
```python
import jax
import jax.numpy as jnp
from jax import lax
from jax.sharding import PartitionSpec as P


def solution(mesh):
    num_ep = mesh.shape['ep']
    row_spec = P(('dp', 'ep'), None)
    replicated = P()
    expert_spec = P('ep', None, None)

    def device_step(tokens, expert_ids, gate_vals, slots, shared_w1, shared_w3, shared_w2, shared_gate, expert_w1, expert_w3, expert_w2):
        tok_count, hidden = tokens.shape
        top_k = expert_ids.shape[1]
        local_experts = expert_w1.shape[0]
        num_experts = local_experts * num_ep
        capacity = 8 * ((2 * tok_count * top_k + 8 * num_experts - 1) // (8 * num_experts))
        buf_rows = num_experts * capacity
        kept_mask = slots >= 0
        slot_dest = jnp.where(kept_mask, expert_ids * capacity + slots, buf_rows)
        copy_tok = jnp.arange(tok_count * top_k, dtype=jnp.int32) // top_k
        row_owner = jnp.full((buf_rows + 1,), tok_count, jnp.int32).at[slot_dest.reshape(-1)].set(copy_tok)
        send_buf = jnp.take(tokens, row_owner[:buf_rows], axis=0, mode='fill', fill_value=0)
        recv_buf = lax.all_to_all(send_buf.reshape(num_ep, local_experts * capacity, hidden), 'ep', 0, 0, tiled=True)
        expert_in = recv_buf.reshape(num_ep, local_experts, capacity, hidden)
        act_a = jnp.einsum('secd,edf->secf', expert_in, expert_w1, preferred_element_type=jnp.float32)
        act_b = jnp.einsum('secd,edf->secf', expert_in, expert_w3, preferred_element_type=jnp.float32)
        hidden_act = (jax.nn.silu(act_a) * act_b).astype(jnp.bfloat16)
        expert_out = jnp.einsum('secf,efd->secd', hidden_act, expert_w2, preferred_element_type=jnp.float32).astype(jnp.bfloat16)
        back_buf = lax.all_to_all(expert_out.reshape(num_ep, local_experts * capacity, hidden), 'ep', 0, 0, tiled=True)
        picked = jnp.take(back_buf.reshape(buf_rows, hidden), slot_dest, axis=0, mode='fill', fill_value=0)
        weights = jnp.where(kept_mask, gate_vals, 0.0)[:, :, None]
        routed = jnp.sum(weights * picked, axis=1)
        gate_logit = jnp.dot(tokens, shared_gate, preferred_element_type=jnp.float32)
        shared_a = jnp.dot(tokens, shared_w1, preferred_element_type=jnp.float32)
        shared_b = jnp.dot(tokens, shared_w3, preferred_element_type=jnp.float32)
        shared_h = (jax.nn.silu(shared_a) * shared_b).astype(jnp.bfloat16)
        shared_out = jnp.dot(shared_h, shared_w2, preferred_element_type=jnp.float32)
        total = tokens.astype(jnp.float32) + jax.nn.sigmoid(gate_logit)[:, None] * shared_out + routed
        return total.astype(jnp.bfloat16)

    return jax.shard_map(device_step, mesh=mesh, in_specs=(row_spec, row_spec, row_spec, row_spec, replicated, replicated, replicated, replicated, expert_spec, expert_spec, expert_spec), out_specs=row_spec, check_vma=False)
```

profile of v0, /device:TPU:103, one launch (start us, length us, event | category | flops | bytes accessed | tf_op | source)
XLA Modules:
  0.0 367.6 jit_solution(8983642750724534745)
XLA Ops:
  0.0 0.0 copy-start
  0.0 0.9 compare_and_fusion.1
  0.9 0.1 copy.16
  1.0 0.1 reshape.60
  1.2 6.2 %scatter_custom_fusion = s32[3073]{0:T(1024)S(1)} fusion(s32[1536]{0:T(1024)S(1)} %fusion.32, s32[1536]{0:T(1024)S(1)} %add_select_fusion, s32[]{:T(128)} %constant.39.clone.1), kind=kCustom, calls=%fused_computation.41 | custom fusion | bytes 12296 | tf_op jit(solution)/shard_map/scatter | solution.py:23
  7.4 0.1 slice.6
  7.5 20.6 %gather_fusion = bf16[3072,1536]{1,0:T(8,128)(2,1)} fusion(bf16[256,1536]{1,0:T(8,128)(2,1)} %param.11, s32[3072]{0:T(1024)S(1)} %get-tuple-element.8), kind=kCustom, calls=%fused_computation | custom fusion | bytes 18886656 | tf_op jit(solution)/shard_map/jit(_take)/gather | solution.py:24
  28.1 8.1 %broadcast_select_fusion = bf16[32,96,1536]{2,1,0:T(8,128)(2,1)} fusion(bf16[32,96,1536]{2,1,0:T(8,128)(2,1)} %bitcast.53, pred[32,96]{1,0:T(8,128)(4,1)S(1)} %compare_and_fusion), kind=kLoop, calls=%fused_computation.5 | loop fusion | flops 4718592 | bytes 18877440 | tf_op jit(solution)/shard_map/jit(_take)/select_n | solution.py:24
  36.1 0.0 copy-start.7
  36.1 121.2 %all_to_all.10 = bf16[32,96,1536]{2,1,0:T(8,128)(2,1)S(1)} all-to-all(bf16[32,96,1536]{2,1,0:T(8,128)(2,1)} %broadcast_select_fusion), channel_id=1, replica_groups=mesh['dp'=1,'ep'=32] {'ep'}, dimensions={0} | all-to-all | bytes 18874368 | tf_op jit(solution)/shard_map/all_to_all | solution.py:25
  157.4 0.0 copy-start.3
  157.4 3.6 copy-done.3
  161.0 0.0 copy-done.7
  161.0 7.0 %fusion = f32[2,32,48,512]{3,2,1,0:T(8,128)} fusion(bf16[32,2,48,1536]{3,2,1,0:T(8,128)(2,1)S(1)} %bitcast.54, bf16[2,1536,512]{2,1,0:T(8,128)(2,1)S(1)} %copy-done.7), kind=kOutput, calls=%fused_computation.6 | convolution fusion | flops 4831838208 | bytes 18874368 | tf_op jit(solution)/shard_map/secd,edf->secf/dot_general | solution.py:28
  168.0 0.0 copy-done
  168.0 16.7 %convert_bitcast_fusion = bf16[32,2,48,1536]{3,2,0,1:T(8,128)(2,1)} fusion(f32[2,32,48,512]{3,2,1,0:T(8,128)} %fusion, bf16[2,512,1536]{2,1,0:T(8,128)(2,1)S(1)} %copy-done, bf16[32,2,48,1536]{3,2,1,0:T(8,128)(2,1)} %bitcast.55, bf16[2,1536,512]{2,1,0:T(8,128)(2,1)} %param.19), kind=kOutput, calls=%fused_computation.4 | convolution fusion | flops 9677832192 | bytes 31457280 | tf_op jit(solution)/shard_map/secf,efd->secd/dot_general | solution.py:30
  184.8 8.2 %copy.18 = bf16[32,2,48,1536]{3,2,1,0:T(8,128)(2,1)} copy(bf16[32,2,48,1536]{3,2,0,1:T(8,128)(2,1)} %convert_bitcast_fusion) | data formatting | bytes 18874368 | tf_op jit(solution)/shard_map/convert_element_type | solution.py:30
  193.0 0.0 copy-start.4
  193.0 0.0 copy-start.5
  193.0 0.0 copy-start.6
  193.0 0.0 copy-start.2
  193.0 6.4 %all-to-all-start.1 = ((bf16[32,96,1536]{2,1,0:T(8,128)(2,1)}), bf16[32,96,1536]{2,1,0:T(8,128)(2,1)}, u32[]{:S(2)}, u32[]{:S(2)}) async-start(bf16[32,96,1536]{2,1,0:T(8,128)(2,1)} %bitcast.52), calls=%async_computation.1 | async-start | bytes 18874368 | tf_op jit(solution)/shard_map/all_to_all | solution.py:31
  199.4 0.1 copy.19
  199.5 0.1 reshape.74
  199.7 0.2 copy.15
  199.9 0.0 copy-done.4
  199.9 0.0 copy-done.5
  199.9 0.1 copy.14
  200.0 0.0 copy-done.6
  200.1 0.0 copy-done.2
  200.1 0.3 fusion.36
  200.4 3.9 %fusion.37 = f32[256,1024]{1,0:T(8,128)} fusion(bf16[256,1536]{1,0:T(8,128)(2,1)S(1)} %copy-done.2, bf16[1536,1024]{1,0:T(8,128)(2,1)} %param.15), kind=kOutput, calls=%fused_computation.54 | convolution fusion | flops 805306368 | bytes 4980736 | tf_op jit(solution)/shard_map/dot_general | solution.py:36
  204.3 123.7 %all-to-all-done.1 = bf16[32,96,1536]{2,1,0:T(8,128)(2,1)} async-done(((bf16[32,96,1536]{2,1,0:T(8,128)(2,1)}), bf16[32,96,1536]{2,1,0:T(8,128)(2,1)}, u32[]{:S(2)}, u32[]{:S(2)}) %all-to-all-start.1) | async-done | bytes 9437216 | tf_op jit(solution)/shard_map/all_to_all | solution.py:31
  328.0 15.3 %gather_fusion.1 = bf16[1536,1536]{1,0:T(8,128)(2,1)} fusion(bf16[3072,1536]{1,0:T(8,128)(2,1)} %bitcast.13, s32[2048]{0:T(1024)S(1)} %pad_clamp_fusion), kind=kCustom, calls=%fused_computation.1 | custom fusion | bytes 9443328 | tf_op jit(solution)/shard_map/jit(_take)/gather | solution.py:32
  343.2 8.3 %reshape.73 = bf16[256,6,1536]{2,1,0:T(8,128)(2,1)} reshape(bf16[1536,1536]{1,0:T(8,128)(2,1)} %gather_fusion.1) | data formatting | bytes 9437184 | tf_op jit(solution)/shard_map/jit(_take)/gather | solution.py:32
  351.5 0.0 copy-start.1
  351.5 9.3 %multiply_reduce_fusion = f32[256,1536]{1,0:T(8,128)} fusion(bf16[256,6,1536]{2,1,0:T(8,128)(2,1)} %reshape.73, f32[256,6]{1,0:T(8,128)S(1)} %copy.14, pred[256,6]{1,0:T(8,128)(4,1)S(1)} %copy.15), kind=kLoop, calls=%fused_computation.3 | loop fusion | flops 9043968 | bytes 6299136 | tf_op jit(solution)/shard_map/reduce_sum | solution.py:34
  360.8 6.7 %fusion.15 = bf16[256,1536]{1,0:T(8,128)(2,1)} fusion(f32[256,1536]{1,0:T(8,128)} %multiply_reduce_fusion, bf16[1024,1536]{1,0:T(8,128)(2,1)} %param.17, bf16[256,1536]{1,0:T(8,128)(2,1)} %param.11, bf16[1536,1024]{1,0:T(8,128)(2,1)} %param.16, f32[256,1024]{1,0:T(8,128)} %fusion.37, f32[256]{0:T(256)S(1)} %add_divide_fusion), kind=kOutput, calls=%fused_computation.24 | convolution fusion | flops 1614151680 | bytes 10486784 | tf_op jit(solution)/shard_map/dot_general | solution.py:39
  367.6 0.0 copy-done.1
  (9 shorter events, 0.1 us)
Async XLA Ops:
  0.0 168.0 %copy-start = (bf16[2,512,1536]{2,1,0:T(8,128)(2,1)S(1)}, bf16[2,512,1536]{2,1,0:T(8,128)(2,1)}, u32[]{:S(2)}) copy-start(bf16[2,512,1536]{2,1,0:T(8,128)(2,1)} %param.21) | copy-start | bytes 9437188
  36.1 124.9 %copy-start.7 = (bf16[2,1536,512]{2,1,0:T(8,128)(2,1)S(1)}, bf16[2,1536,512]{2,1,0:T(8,128)(2,1)}, u32[]{:S(2)}) copy-start(bf16[2,1536,512]{2,1,0:T(8,128)(2,1)} %param.20) | copy-start | bytes 9437188
  157.4 3.6 copy-start.3
  193.0 6.9 %copy-start.4 = (s32[256,6]{0,1:T(8,128)S(1)}, s32[256,6]{0,1:T(8,128)}, u32[]{:S(2)}) copy-start(s32[256,6]{0,1:T(8,128)} %param.14) | copy-start | bytes 18436
  193.0 6.9 %copy-start.5 = (f32[256,6]{0,1:T(8,128)S(1)}, f32[256,6]{0,1:T(8,128)}, u32[]{:S(2)}) copy-start(f32[256,6]{0,1:T(8,128)} %param.13) | copy-start | bytes 18436
  193.0 7.1 %copy-start.6 = (bf16[1536]{0:T(1024)(128)(2,1)S(1)}, bf16[1536]{0:T(1024)(128)(2,1)}, u32[]{:S(2)}) copy-start(bf16[1536]{0:T(1024)(128)(2,1)} %param.18) | copy-start | bytes 9220
  193.0 7.1 %copy-start.2 = (bf16[256,1536]{1,0:T(8,128)(2,1)S(1)}, bf16[256,1536]{1,0:T(8,128)(2,1)}, u32[]{:S(2)}) copy-start(bf16[256,1536]{1,0:T(8,128)(2,1)} %param.11) | copy-start | bytes 2359300
  193.0 135.0 %all-to-all-start.1 = ((bf16[32,96,1536]{2,1,0:T(8,128)(2,1)}), bf16[32,96,1536]{2,1,0:T(8,128)(2,1)}, u32[]{:S(2)}, u32[]{:S(2)}) async-start(bf16[32,96,1536]{2,1,0:T(8,128)(2,1)} %bitcast.52), calls=%async_computation.1 | async-start | bytes 18874368 | tf_op jit(solution)/shard_map/all_to_all | solution.py:31
  351.5 16.1 %copy-start.1 = (bf16[2,512,1536]{2,1,0:T(8,128)(2,1)S(1)}, bf16[2,512,1536]{2,1,0:T(8,128)(2,1)}, u32[]{:S(2)}) copy-start(bf16[2,512,1536]{2,1,0:T(8,128)(2,1)} %param.21) | copy-start | bytes 9437188
where the time goes:
time: 368 us
  waiting for transfers between devices  124 us (34%)
  blocking collectives  121 us (33%)
  local copies, waits for them, and re-layouts  63.1 us (17%)
  matrix products  34.7 us (9%)
  other arithmetic  18.3 us (5%)
  starting transfers between devices  6.39 us (2%)
    all_to_all x1, waiting for transfers between devices, device_step(): lax.all_to_all(expert_out.reshape(num_ep, local_experts * capacity, hidde...  124 us
    all_to_all x1, blocking collectives, device_step(): lax.all_to_all(send_buf.reshape(num_ep, local_experts * capacity, hidden)...  121 us
    gather x2, local copies, waits for them, and re-layouts, device_step(): jnp.take(back_buf.reshape(buf_rows, hidden), slot_dest, axis=0, mode='fil...  23.6 us
    gather x1, local copies, waits for them, and re-layouts, device_step(): jnp.take(tokens, row_owner[:buf_rows], axis=0, mode='fill', fill_value=0)  20.6 us
    dot_general x1, matrix products, device_step(): jnp.einsum('secf,efd->secd', hidden_act, expert_w2, preferred_element_typ...  16.7 us
    reduce_sum x1, other arithmetic, device_step(): routed = jnp.sum(weights * picked, axis=1)  9.31 us
    convert_element_type x1, local copies, waits for them, and re-layouts, device_step(): jnp.einsum('secf,efd->secd', hidden_act, expert_w2, preferred_element_typ...  8.2 us
    select_n x1, other arithmetic, device_step(): jnp.take(tokens, row_owner[:buf_rows], axis=0, mode='fill', fill_value=0)  8.06 us
  transfers between devices with their start and end apart: 1, of which 1 were waited for; matrix products, arithmetic and copies ran while one was open for 1% of the time, Pallas kernels for 0%

commit v1 on v0

v1 whole, which is shorter than its diff:
```python
import functools
import math

import jax
import jax.numpy as jnp
from jax import lax
from jax.experimental import pallas as pl
from jax.experimental.pallas import tpu as pltpu
from jax.sharding import PartitionSpec as P

MESH = pl.DeviceIdType.MESH
VMEM_LIMIT = 67043328
F32, BF16 = jnp.float32, jnp.bfloat16

DIRS = ((0, 1), (0, -1), (1, 1), (1, -1))


def wrap(v):
    return (v + 1) % 4 - 1


def shift(axis, way, at):
    moved = list(at)
    moved[axis] = wrap(moved[axis] - way)
    return tuple(moved)


def ahead_piece(way):
    return 0 if way > 0 else 1


def plan_gather():
    queues = [[] for _ in DIRS]
    first = []
    for d, (axis, way) in enumerate(DIRS):
        for half in (axis, 1 - axis):
            for p in (ahead_piece(way), 1 - ahead_piece(way)):
                queues[d].append((half, (0, 0), p))
                first.append((d, (half, (0, 0), p)))
    steps = []
    while any(queues):
        moved = [q.pop(0) if q else None for q in queues]
        arrivals = []
        for d, piece in enumerate(moved):
            if piece is None:
                continue
            half, at, p = piece
            axis, way = DIRS[d]
            at = shift(axis, way, at)
            onward = []
            if p == ahead_piece(way) and abs(at[axis]) == 1:
                onward.append(d)
            if axis == half:
                onward += [e for e, (other, _) in enumerate(DIRS) if other != axis]
            for e in onward:
                queues[e].append((half, at, p))
            arrivals.append((d, (half, at, p), onward))
        steps.append(arrivals)
    return first, steps


def plan_units(steps, chips_per_unit=2):
    done = {(0, 0): 0}
    for i, arrivals in enumerate(steps):
        for _, (_, at, _), _ in arrivals:
            done[at] = i + 1
    order = sorted(done, key=lambda at: (done[at], at))
    units = [order[i : i + chips_per_unit] for i in range(0, len(order), chips_per_unit)]
    return units, [max(done[at] for at in unit) for unit in units]


def carries_meta(piece):
    half, _, p = piece
    return half == 0 and p == 0


def place(side):
    me = lax.axis_index('ep')
    chip = me // 2
    return me, lax.rem(chip, side), chip // side, lax.rem(me, 2)


def pick(table, i):
    out = i * 0 + table[0]
    for k in range(1, len(table)):
        out = jnp.where(i == k, table[k], out)
    return out


def silu_gate(a, b):
    return (jax.nn.silu(a) * b).astype(BF16)


def gather_kernel(side, capacity, top_k, tok_in, meta_in, sw1_in, sw3_in, sw2_in, sg_ref, w1_in, w3_in, w2_in,
                  r_out, meta, base,
                  tok, w1, w3, w2, sw1, sw3, sw2, xe, rows_out,
                  load_sem, link_send, chip_send, recv, meta_link_send, meta_chip_send, meta_recv, out_sem):
    me, x, y, c = place(side)
    first, steps = plan_gather()
    units, ready = plan_units(steps)
    link_order = [[piece for e, piece in first if e == d] for d in range(4)]
    chip_order = [(half, (0, 0), p) for half in range(2) for p in range(2)]
    for arrivals in steps:
        for _, piece, onward in arrivals:
            chip_order.append(piece)
            for e in onward:
                link_order[e].append(piece)
    meta_order = [[piece for piece in link_order[d] if carries_meta(piece)] for d in range(4)]
    meta_chip_order = [piece for piece in chip_order if carries_meta(piece)]
    n_tok, hidden = tok_in.shape
    half_cols, half_rows = hidden // 2, n_tok // 2
    pair = 2 * capacity

    def device(at, core=None):
        dx, dy = at
        col, row = lax.rem(x + (dx + side), side), lax.rem(y + (dy + side), side)
        return (row * side + col) * 2 + (c if core is None else core)

    def neighbour(d):
        axis, way = DIRS[d]
        return device((way, 0) if axis == 0 else (0, way))

    partner = me + 1 - 2 * c

    loads = [pltpu.make_async_copy(tok_in, tok.at[me], load_sem.at[0]),
             pltpu.make_async_copy(meta_in, meta.at[me], load_sem.at[1]),
             pltpu.make_async_copy(sw1_in, sw1, load_sem.at[2]),
             pltpu.make_async_copy(sw3_in, sw3, load_sem.at[3]),
             pltpu.make_async_copy(sw2_in, sw2, load_sem.at[4]),
             pltpu.make_async_copy(w1_in, w1, load_sem.at[5]),
             pltpu.make_async_copy(w3_in, w3, load_sem.at[6]),
             pltpu.make_async_copy(w2_in, w2, load_sem.at[7])]
    for load in loads:
        load.start()

    barrier = pltpu.get_barrier_semaphore()
    for to in [neighbour(d) for d in range(4)] + [partner]:
        pl.semaphore_signal(barrier, inc=1, device_id={'ep': to}, device_id_type=MESH)
    pl.semaphore_wait(barrier, 5)
    loads[0].wait()
    loads[1].wait()

    def view(half, src, p):
        return tok.at[src, pl.ds(p * half_rows, half_rows), pl.ds(half * half_cols, half_cols)]

    def rdma(src, dst, send, arrive, to):
        return pltpu.make_async_remote_copy(src_ref=src, dst_ref=dst, send_sem=send, recv_sem=arrive,
                                            device_id={'ep': to}, device_id_type=MESH)

    def piece_copy(piece, src, send, to):
        half, _, p = piece
        return rdma(view(half, src, p), view(half, src, p), send, recv.at[src, half * 2 + p], to)

    def meta_copy(src, send, to):
        return rdma(meta.at[src], meta.at[src], send, meta_recv.at[src], to)

    def send_link(d, piece):
        src = device(piece[1])
        piece_copy(piece, src, link_send.at[d, link_order[d].index(piece)], neighbour(d)).start()
        if carries_meta(piece):
            meta_copy(src, meta_link_send.at[d, meta_order[d].index(piece)], neighbour(d)).start()

    def send_chip(piece):
        src = device(piece[1])
        piece_copy(piece, src, chip_send.at[chip_order.index(piece)], partner).start()
        if carries_meta(piece):
            meta_copy(src, meta_chip_send.at[meta_chip_order.index(piece)], partner).start()

    def await_piece(piece, core):
        src = device(piece[1], core)
        piece_copy(piece, src, link_send.at[0, 0], partner).wait_recv()
        if carries_meta(piece):
            meta_copy(src, meta_link_send.at[0, 0], partner).wait_recv()

    def do_step(i):
        for d, piece, onward in steps[i]:
            await_piece(piece, None)
            for e in onward:
                send_link(e, piece)
            send_chip(piece)

    for d, piece in first:
        send_link(d, piece)
    for half in range(2):
        for p in range(2):
            send_chip((half, (0, 0), p))

    for load in loads[2:5]:
        load.wait()
    x_own = tok[me]
    tile = 256
    base[...] = jnp.zeros_like(base)

    def shared_tile(n, _):
        cols = pl.ds(pl.multiple_of(n * tile, tile), tile)
        a = jnp.dot(x_own, sw1[:, cols], preferred_element_type=F32)
        b = jnp.dot(x_own, sw3[:, cols], preferred_element_type=F32)
        base[...] += jnp.dot(silu_gate(a, b), sw2[cols, :], preferred_element_type=F32)
        return 0

    lax.fori_loop(0, sw1.shape[1] // tile, shared_tile, 0)
    x_f32 = x_own.astype(F32)
    logit = jnp.sum(x_f32 * sg_ref[...].astype(F32), axis=1, keepdims=True)
    base[...] = x_f32 + jax.nn.sigmoid(logit) * base[...]
    for load in loads[5:]:
        load.wait()

    row_ids = lax.broadcasted_iota(jnp.int32, (pair, n_tok), 0)
    target = (row_ids + me * pair).astype(F32)
    n_src = 4

    def unit_device(u, i):
        dx = pick([unit[i // 2][0] + side for unit in units], u)
        dy = pick([unit[i // 2][1] + side for unit in units], u)
        col, row = lax.rem(x + dx, side), lax.rem(y + dy, side)
        return (row * side + col) * 2 + i % 2

    def out_copies(slot, srcs):
        return [pltpu.make_async_copy(
                    rows_out.at[slot, j, pl.ds(i * capacity, capacity), pl.ds(h * half_cols, half_cols)],
                    r_out.at[h, srcs[i], pl.ds(j * capacity, capacity)],
                    out_sem.at[slot, (i * 2 + j) * 2 + h])
                for i in range(n_src) for j in range(2) for h in range(2)]

    def do_unit(u, _):
        done = 0
        for k, after in enumerate(ready):
            lo, hi = done, after
            done = after

            @pl.when(u == k)
            def _(lo=lo, hi=hi, k=k):
                for i in range(lo, hi):
                    do_step(i)
                for at in units[k]:
                    for half in range(2):
                        for p in range(2):
                            await_piece((half, at, p), 1 - c)

        slot = lax.rem(u, 2)
        srcs = [unit_device(u, i) for i in range(n_src)]

        @pl.when(u >= 2)
        def _():
            for copy in out_copies(slot, srcs):
                copy.wait()

        for i in range(n_src):
            codes = meta[srcs[i], 0:8, :]
            hit = codes[0:1, :] == target
            for k in range(1, top_k):
                hit = jnp.logical_or(hit, codes[k : k + 1, :] == target)
            one_hot = jnp.where(hit, 1.0, 0.0).astype(BF16)
            picked = jnp.dot(one_hot, tok[srcs[i]], preferred_element_type=F32).astype(BF16)
            xe[0, i * capacity : (i + 1) * capacity, :] = picked[:capacity]
            xe[1, i * capacity : (i + 1) * capacity, :] = picked[capacity:]

        def do_expert(j, _):
            a = jnp.dot(xe[j], w1[j], preferred_element_type=F32)
            b = jnp.dot(xe[j], w3[j], preferred_element_type=F32)
            rows_out[slot, j] = jnp.dot(silu_gate(a, b), w2[j], preferred_element_type=F32).astype(BF16)
            return 0

        lax.fori_loop(0, 2, do_expert, 0)
        for copy in out_copies(slot, srcs):
            copy.start()
        return 0

    n_units = len(units)
    lax.fori_loop(0, n_units, do_unit, 0)
    for u in range(n_units - 2, n_units):
        for copy in out_copies(u % 2, [me] * n_src):
            copy.wait()
    for d in range(4):
        for i, piece in enumerate(link_order[d]):
            piece_copy(piece, me, link_send.at[d, i], partner).wait_send()
        for i in range(len(meta_order[d])):
            meta_copy(me, meta_link_send.at[d, i], partner).wait_send()
    for i, piece in enumerate(chip_order):
        piece_copy(piece, me, chip_send.at[i], partner).wait_send()
    for i in range(len(meta_chip_order)):
        meta_copy(me, meta_chip_send.at[i], partner).wait_send()


def return_kernel(side, capacity, top_k, r_in, meta, base, y_out,
                  rows, relay, wt, part, hop1, hop2,
                  direct_send, relay_send, fwd_send, chip_send, local_sem, rows_recv, relay_recv,
                  hop1_send, hop1_recv, hop2_send, hop2_recv):
    me, x, y, c = place(side)
    n_tok = base.shape[0]
    half_cols, half_rows = base.shape[1] // 2, n_tok // 2
    pair = 2 * capacity
    order = (2, 1, -1, 0)

    def device(dx, dy, core):
        col, row = lax.rem(x + (dx + side), side), lax.rem(y + (dy + side), side)
        return (row * side + col) * 2 + core

    def along(h, a, b, core):
        return device(a, b, core) if h == 0 else device(b, a, core)

    partner = me + 1 - 2 * c
    here = (x, y)

    barrier = pltpu.get_barrier_semaphore()
    peers = [along(h, w, 0, core) for h in range(2) for w in (1, -1) for core in range(2)] + [partner]
    for to in peers:
        pl.semaphore_signal(barrier, inc=1, device_id={'ep': to}, device_id_type=MESH)
    pl.semaphore_wait(barrier, len(peers))

    def rdma(src, dst, send, arrive, to):
        return pltpu.make_async_remote_copy(src_ref=src, dst_ref=dst, send_sem=send, recv_sem=arrive,
                                            device_id={'ep': to}, device_id_type=MESH)

    def go(copy):
        copy.start()

    def entry(h, hops, core):
        return lax.rem(here[h] + (hops + side), side) * 2 + core

    def send_chunk(q):
        for h in range(2):
            b = order[q]
            for w, way in enumerate((1, -1)):
                go(rdma(r_in.at[h, along(h, 2, b, w)], relay.at[h, q, w], relay_send.at[h, q, w], relay_recv.at[h, q, w],
                        along(h, way, 0, c)))
        for h in range(2):
            b = order[q]
            mine = entry(h, 0, c)
            for w, way in enumerate((1, -1)):
                for core in range(2):
                    go(rdma(r_in.at[h, along(h, way, b, core)], rows.at[h, q, mine], direct_send.at[h, q, w * 2 + core],
                            rows_recv.at[h, q, mine], along(h, way, 0, core)))
            go(rdma(r_in.at[h, along(h, 0, b, 1 - c)], rows.at[h, q, mine], chip_send.at[h, q], rows_recv.at[h, q, mine],
                    partner))
            own = pltpu.make_async_copy(r_in.at[h, along(h, 0, b, c)], rows.at[h, q, mine], local_sem.at[h, q])
            own.start()

    def forward(q):
        for h in range(2):
            for w, way in enumerate((1, -1)):
                rdma(relay.at[h, q, w], relay.at[h, q, w], relay_send.at[h, q, w], relay_recv.at[h, q, w],
                     partner).wait_recv()
                src = entry(h, -way, c)
                go(rdma(relay.at[h, q, w], rows.at[h, q, src], fwd_send.at[h, q, w], rows_recv.at[h, q, src],
                        along(h, way, 0, w)))

    def await_rows(h, q):
        mine = entry(h, 0, c)
        pltpu.make_async_copy(r_in.at[h, me], rows.at[h, q, mine], local_sem.at[h, q]).wait()
        for hops in (0, 1, -1, 2):
            for core in range(2):
                if hops == 0:
                    if core == 1:
                        continue
                    src = entry(h, 0, 1 - c)
                else:
                    src = entry(h, hops, core)
                rdma(r_in.at[h, me], rows.at[h, q, src], chip_send.at[h, q], rows_recv.at[h, q, src], partner).wait_recv()

    def second(h, way):
        return along(h, 0, way, c)

    def hop1_copy(h, w):
        way = (1, -1)[w]
        return rdma(part.at[h, 0, pl.ds(w * half_rows, half_rows)], hop1.at[h, w], hop1_send.at[h, w], hop1_recv.at[h, w],
                    second(h, way))

    def hop2_copy(h, w, p):
        way = (1, -1)[w]
        piece = pl.ds(p * half_rows, half_rows)
        return rdma(part.at[h, 1 + w, piece], hop2.at[h, w, piece], hop2_send.at[h, w, p], hop2_recv.at[h, w, p],
                    second(h, way))

    send_chunk(0)
    send_chunk(1)

    row_ids = lax.broadcasted_iota(jnp.int32, (pair, n_tok), 0)

    def combine(n, _):
        q, h = n // 2, lax.rem(n, 2)
        for k in range(4):
            @pl.when(n == 2 * k)
            def _(k=k):
                forward(k)
                if k + 2 < 4:
                    send_chunk(k + 2)
            for hh in range(2):
                @pl.when(n == 2 * k + hh)
                def _(k=k, hh=hh):
                    await_rows(hh, k)
        b = pick([o + side for o in order], q)
        bx, by = lax.rem(x + jnp.where(h == 0, 0, b), side), lax.rem(y + jnp.where(h == 0, b, 0), side)
        dest = (by * side + bx) * 2 + c
        codes = meta[dest, 0:8, :]
        gates = meta[dest, 8:16, :]

        def weights(g, _):
            gx, gy = jnp.where(h == 0, g // 2, x), jnp.where(h == 0, y, g // 2)
            source = (gy * side + gx) * 2 + lax.rem(g, 2)
            target = (row_ids + source * pair).astype(F32)
            w = jnp.where(codes[0:1, :] == target, gates[0:1, :], 0.0)
            for k in range(1, top_k):
                w = jnp.where(codes[k : k + 1, :] == target, gates[k : k + 1, :], w)
            at = pl.ds(pl.multiple_of(g * pair, pair), pair)
            hi = w.astype(BF16)
            w = w - hi.astype(F32)
            mid = w.astype(BF16)
            wt[0, at, :] = hi
            wt[1, at, :] = mid
            wt[2, at, :] = (w - mid.astype(F32)).astype(BF16)
            return 0

        lax.fori_loop(0, 2 * side, weights, 0)
        block = rows[h, q].reshape(2 * side * pair, half_cols)
        dims = (((0,), (0,)), ((), ()))
        total = lax.dot_general(wt[2], block, dims, preferred_element_type=F32)
        total += lax.dot_general(wt[1], block, dims, preferred_element_type=F32)
        total += lax.dot_general(wt[0], block, dims, preferred_element_type=F32)
        part[h, q] = total

        for hh in range(2):
            @pl.when(n == hh)
            def _(hh=hh):
                for w in range(2):
                    hop1_copy(hh, w).start()
            for w in range(2):
                @pl.when(n == 2 * (1 + w) + hh)
                def _(hh=hh, w=w):
                    hop2_copy(hh, w, 1 - w).start()
                    hop1_copy(hh, w).wait_recv()
                    own = pl.ds(w * half_rows, half_rows)
                    part[hh, 1 + w, own] += hop1[hh, w]
                    hop2_copy(hh, w, w).start()
        return 0

    lax.fori_loop(0, 8, combine, 0)
    for h in range(2):
        for w in range(2):
            for p in range(2):
                hop2_copy(h, w, p).wait_recv()
        cols = slice(h * half_cols, (h + 1) * half_cols)
        y_out[:, cols] = (base[:, cols] + (part[h, 3] + (hop2[h, 0] + hop2[h, 1]))).astype(BF16)
    for h in range(2):
        for q in range(4):
            sems = [relay_send.at[h, q, w] for w in range(2)] + [fwd_send.at[h, q, w] for w in range(2)]
            sems += [direct_send.at[h, q, k] for k in range(4)] + [chip_send.at[h, q]]
            for sem in sems:
                rdma(r_in.at[h, me], rows.at[h, q, 0], sem, rows_recv.at[h, q, 0], partner).wait_send()
        for w in range(2):
            hop1_copy(h, w).wait_send()
            for p in range(2):
                hop2_copy(h, w, p).wait_send()


def solution(mesh):
    num_ep = mesh.shape['ep']
    side = math.isqrt(num_ep // 2)
    assert side == 4 and 2 * side * side == num_ep
    row_spec = P(('dp', 'ep'), None)
    replicated = P()
    expert_spec = P('ep', None, None)
    vmem, anywhere = pl.BlockSpec(memory_space=pltpu.VMEM), pl.BlockSpec(memory_space=pl.ANY)
    dma = pltpu.SemaphoreType.DMA

    def device_step(tokens, expert_ids, gate_vals, slots, shared_w1, shared_w3, shared_w2, shared_gate, expert_w1, expert_w3, expert_w2):
        tok_count, hidden = tokens.shape
        top_k = expert_ids.shape[1]
        local_experts, _, ff = expert_w1.shape
        num_experts = local_experts * num_ep
        capacity = 8 * ((2 * tok_count * top_k + 8 * num_experts - 1) // (8 * num_experts))
        assert local_experts == 2 and top_k <= 8 and capacity % 16 == 0
        pair = local_experts * capacity
        half = hidden // 2
        code = jnp.where(slots >= 0, expert_ids * capacity + slots, -1).astype(F32)
        pad = ((0, 0), (0, 8 - top_k))
        meta = jnp.concatenate([jnp.pad(code, pad, constant_values=-1.0), jnp.pad(gate_vals, pad)], axis=1).T
        r, meta_all, base = pl.pallas_call(
            functools.partial(gather_kernel, side, capacity, top_k),
            out_shape=(jax.ShapeDtypeStruct((2, num_ep, pair, half), BF16),
                       jax.ShapeDtypeStruct((num_ep, 16, tok_count), F32),
                       jax.ShapeDtypeStruct((tok_count, hidden), F32)),
            in_specs=[anywhere] * 5 + [vmem] + [anywhere] * 3,
            out_specs=(anywhere, vmem, vmem),
            scratch_shapes=[
                pltpu.VMEM((num_ep, tok_count, hidden), BF16),
                pltpu.VMEM((local_experts, hidden, ff), BF16),
                pltpu.VMEM((local_experts, hidden, ff), BF16),
                pltpu.VMEM((local_experts, ff, hidden), BF16),
                pltpu.VMEM(shared_w1.shape, BF16),
                pltpu.VMEM(shared_w3.shape, BF16),
                pltpu.VMEM(shared_w2.shape, BF16),
                pltpu.VMEM((local_experts, 4 * capacity, hidden), BF16),
                pltpu.VMEM((2, local_experts, 4 * capacity, hidden), BF16),
                dma((8,)), dma((4, 15)), dma((64,)), dma((num_ep, 4)), dma((4, 15)), dma((16,)), dma((num_ep,)),
                dma((2, 16)),
            ],
            compiler_params=pltpu.CompilerParams(collective_id=0, has_side_effects=True, vmem_limit_bytes=VMEM_LIMIT),
            name='gather_experts',
        )(tokens, meta, shared_w1, shared_w3, shared_w2, shared_gate.reshape(1, hidden), expert_w1, expert_w3, expert_w2)
        return pl.pallas_call(
            functools.partial(return_kernel, side, capacity, top_k),
            out_shape=jax.ShapeDtypeStruct((tok_count, hidden), BF16),
            in_specs=[anywhere, vmem, vmem],
            out_specs=vmem,
            scratch_shapes=[
                pltpu.VMEM((2, 4, 2 * side, pair, half), BF16),
                pltpu.VMEM((2, 4, 2, pair, half), BF16),
                pltpu.VMEM((3, 2 * side * pair, tok_count), BF16),
                pltpu.VMEM((2, 4, tok_count, half), F32),
                pltpu.VMEM((2, 2, tok_count // 2, half), F32),
                pltpu.VMEM((2, 2, tok_count, half), F32),
                dma((2, 4, 4)), dma((2, 4, 2)), dma((2, 4, 2)), dma((2, 4)), dma((2, 4)), dma((2, 4, 2 * side)),
                dma((2, 4, 2)), dma((2, 2)), dma((2, 2)), dma((2, 2, 2)), dma((2, 2, 2)),
            ],
            compiler_params=pltpu.CompilerParams(collective_id=1, has_side_effects=True, vmem_limit_bytes=VMEM_LIMIT),
            name='return_combine',
        )(r, meta_all, base)

    return jax.shard_map(device_step, mesh=mesh, in_specs=(row_spec, row_spec, row_spec, row_spec, replicated, replicated, replicated, replicated, expert_spec, expert_spec, expert_spec), out_specs=row_spec, check_vma=False)
```

time: 368 us -> 198 us (0.54)
  the two profiles are of different devices: /device:TPU:103 before, /device:TPU:97 now
where the time goes in v1:
time: 198 us
  Pallas kernels  192 us (97%)
  local copies, waits for them, and re-layouts  3.35 us (2%)
  other arithmetic  2.03 us (1%)
    pallas_call x1, Pallas kernels, device_step(): pl.pallas_call(functools.partial(return_kernel, side, capacity, top_k), o...  102 us
    pallas_call x1, Pallas kernels, device_step(): pl.pallas_call(functools.partial(gather_kernel, side, capacity, top_k), o...  90.6 us

profile of v1, /device:TPU:97, one launch (start us, length us, event | category | flops | bytes accessed | tf_op | source)
XLA Modules:
  0.0 197.7 jit_solution(5235848402294949907)
XLA Ops:
  0.0 1.3 reshape.3.sg_ref
  1.3 0.7 select_convert_fusion
  2.0 1.3 fusion.meta_in
  3.3 90.6 %gather_experts.1 = (bf16[2,32,96,768]{3,2,1,0:T(8,128)(2,1)}, f32[32,16,256]{2,1,0:T(8,128)}, f32[256,1536]{1,0:T(8,128)}) custom-call(bf16[256,1536]{1,0:T(8,128)(2,1)} %tok_in.1, f32[16,256]{1,0:T(8,128)} %fusion.meta_in, bf16[1536,1024]{1,0:T(8,128)(2,1)} %sw1_in.1, bf16[1536,1024]{1,0:T(8,128)(2,1)} %sw3_in.1, bf16[1024,1536]{1,0:T(8,128)(2,1)} %sw2_in.1, ...), custom_call_target="tpu_custom_call" | custom-call | tf_op jit(solution)/shard_map/gather_experts/pallas_call | solution.py:478
  93.9 101.8 %return_combine.1 = bf16[256,1536]{1,0:T(8,128)(2,1)} custom-call(bf16[2,32,96,768]{3,2,1,0:T(8,128)(2,1)} %get-tuple-element.8.r_in, f32[32,16,256]{2,1,0:T(8,128)} %get-tuple-element.9.meta, f32[256,1536]{1,0:T(8,128)} %get-tuple-element.10.base), custom_call_target="tpu_custom_call" | custom-call | tf_op jit(solution)/shard_map/return_combine/pallas_call | solution.py:501
  195.7 2.1 %copy.13 = bf16[256,1536]{1,0:T(8,128)(2,1)} copy(bf16[256,1536]{1,0:T(8,128)(2,1)} %return_combine.1) | data formatting | bytes 1572864

commit v2 on v1

v2 whole, which is shorter than its diff:
```python
import functools
import math

import jax
import jax.numpy as jnp
from jax import lax
from jax.experimental import pallas as pl
from jax.experimental.pallas import tpu as pltpu
from jax.sharding import PartitionSpec as P

MESH = pl.DeviceIdType.MESH
VMEM_LIMIT = 67043328
F32, BF16 = jnp.float32, jnp.bfloat16

DIRS = ((0, 1), (0, -1), (1, 1), (1, -1))


def wrap(v):
    return (v + 1) % 4 - 1


def shift(axis, way, at):
    moved = list(at)
    moved[axis] = wrap(moved[axis] - way)
    return tuple(moved)


def ahead_piece(way):
    return 0 if way > 0 else 1


def plan_gather():
    queues = [[] for _ in DIRS]
    first = []
    for d, (axis, way) in enumerate(DIRS):
        for half in (axis, 1 - axis):
            for p in (ahead_piece(way), 1 - ahead_piece(way)):
                queues[d].append((half, (0, 0), p))
                first.append((d, (half, (0, 0), p)))
    steps = []
    while any(queues):
        moved = [q.pop(0) if q else None for q in queues]
        arrivals = []
        for d, piece in enumerate(moved):
            if piece is None:
                continue
            half, at, p = piece
            axis, way = DIRS[d]
            at = shift(axis, way, at)
            onward = []
            if p == ahead_piece(way) and abs(at[axis]) == 1:
                onward.append(d)
            if axis == half:
                onward += [e for e, (other, _) in enumerate(DIRS) if other != axis]
            for e in onward:
                queues[e].append((half, at, p))
            arrivals.append((d, (half, at, p), onward))
        steps.append(arrivals)
    return first, steps


def plan_units(steps, chips_per_unit=2):
    done = {(0, 0): 0}
    for i, arrivals in enumerate(steps):
        for _, (_, at, _), _ in arrivals:
            done[at] = i + 1
    order = sorted(done, key=lambda at: (done[at], at))
    units = [order[i : i + chips_per_unit] for i in range(0, len(order), chips_per_unit)]
    return units, [max(done[at] for at in unit) for unit in units]


def carries_meta(piece):
    half, _, p = piece
    return half == 0 and p == 0


def place(side):
    me = lax.axis_index('ep')
    chip = me // 2
    return me, lax.rem(chip, side), chip // side, lax.rem(me, 2)


def pick(table, i):
    out = i * 0 + table[0]
    for k in range(1, len(table)):
        out = jnp.where(i == k, table[k], out)
    return out


def silu_gate(a, b):
    return (jax.nn.silu(a) * b).astype(BF16)


def layer_kernel(side, capacity, tok_in, ids_ref, slots_ref, gates_ref, sw1_in, sw3_in, sw2_in, sg_ref, w1_in, w3_in, w2_in,
                 y_out, r_buf, relay,
                 tok, meta, base, w1, w3, w2, xe, rows, wt, part, hop1, hop2,
                 load_sem, link_send, chip_send, recv, meta_link_send, meta_chip_send, meta_recv, out_sem,
                 direct_send, relay_send, fwd_send, pair_send, local_sem, rows_recv, relay_recv,
                 hop1_send, hop1_recv, hop2_send, hop2_recv):
    me, x, y, c = place(side)
    first, steps = plan_gather()
    units, ready = plan_units(steps)
    link_order = [[piece for e, piece in first if e == d] for d in range(4)]
    chip_order = [(half, (0, 0), p) for half in range(2) for p in range(2)]
    for arrivals in steps:
        for _, piece, onward in arrivals:
            chip_order.append(piece)
            for e in onward:
                link_order[e].append(piece)
    meta_order = [[piece for piece in link_order[d] if carries_meta(piece)] for d in range(4)]
    meta_chip_order = [piece for piece in chip_order if carries_meta(piece)]
    top_k = ids_ref.shape[0]
    n_tok, hidden = tok_in.shape
    half_cols, half_rows = hidden // 2, n_tok // 2
    ff = w1.shape[2]
    pair = 2 * capacity
    here = (x, y)

    def device(at, core=None):
        dx, dy = at
        col, row = lax.rem(x + (dx + side), side), lax.rem(y + (dy + side), side)
        return (row * side + col) * 2 + (c if core is None else core)

    def along(h, a, b, core):
        return device((a, b) if h == 0 else (b, a), core)

    def neighbour(d, core=None):
        axis, way = DIRS[d]
        return device((way, 0) if axis == 0 else (0, way), core)

    def rdma(src, dst, send, arrive, to):
        return pltpu.make_async_remote_copy(src_ref=src, dst_ref=dst, send_sem=send, recv_sem=arrive,
                                            device_id={'ep': to}, device_id_type=MESH)

    partner = me + 1 - 2 * c

    tok_load = pltpu.make_async_copy(tok_in, tok.at[me], load_sem.at[0])
    tok_load.start()
    shared_loads, expert_loads = [], []
    for j in range(2):
        cols = pl.ds(j * ff, ff)
        shared_loads += [pltpu.make_async_copy(sw1_in.at[:, cols], w1.at[j], load_sem.at[1 + j]),
                         pltpu.make_async_copy(sw3_in.at[:, cols], w3.at[j], load_sem.at[3 + j]),
                         pltpu.make_async_copy(sw2_in.at[cols], w2.at[j], load_sem.at[5 + j])]
    for k, (src, dst) in enumerate(((w1_in, w1), (w3_in, w3), (w2_in, w2))):
        expert_loads.append(pltpu.make_async_copy(src, dst, load_sem.at[7 + k]))
    for load in shared_loads:
        load.start()

    barrier = pltpu.get_barrier_semaphore()
    for to in [neighbour(d, core) for d in range(4) for core in range(2)] + [partner]:
        pl.semaphore_signal(barrier, inc=1, device_id={'ep': to}, device_id_type=MESH)
    slot_of = slots_ref[...]
    meta[me, 0:top_k, :] = jnp.where(slot_of >= 0, ids_ref[...] * capacity + slot_of, -1).astype(F32)
    meta[me, 8 : 8 + top_k, :] = gates_ref[...]
    meta[me, top_k:8, :] = jnp.full((8 - top_k, n_tok), -1.0, F32)
    meta[me, 8 + top_k : 16, :] = jnp.zeros((8 - top_k, n_tok), F32)
    tok_load.wait()
    pl.semaphore_wait(barrier, 9)

    def view(half, src, p):
        return tok.at[src, pl.ds(p * half_rows, half_rows), pl.ds(half * half_cols, half_cols)]

    def piece_copy(piece, src, send, to):
        half, _, p = piece
        return rdma(view(half, src, p), view(half, src, p), send, recv.at[src, half * 2 + p], to)

    def meta_copy(src, send, to):
        return rdma(meta.at[src], meta.at[src], send, meta_recv.at[src], to)

    def send_link(d, piece):
        src = device(piece[1])
        piece_copy(piece, src, link_send.at[d, link_order[d].index(piece)], neighbour(d)).start()
        if carries_meta(piece):
            meta_copy(src, meta_link_send.at[d, meta_order[d].index(piece)], neighbour(d)).start()

    def send_chip(piece):
        src = device(piece[1])
        piece_copy(piece, src, chip_send.at[chip_order.index(piece)], partner).start()
        if carries_meta(piece):
            meta_copy(src, meta_chip_send.at[meta_chip_order.index(piece)], partner).start()

    def await_piece(piece, core):
        src = device(piece[1], core)
        piece_copy(piece, src, link_send.at[0, 0], partner).wait_recv()
        if carries_meta(piece):
            meta_copy(src, meta_link_send.at[0, 0], partner).wait_recv()

    def do_step(i):
        for d, piece, onward in steps[i]:
            await_piece(piece, None)
            for e in onward:
                send_link(e, piece)
            send_chip(piece)

    order = (2, 1, -1, 0)

    def entry(h, hops, core):
        return lax.rem(here[h] + (hops + side), side) * 2 + core

    def send_relay(q):
        for h in range(2):
            for w, way in enumerate((1, -1)):
                rdma(r_buf.at[h, along(h, 2, order[q], w)], relay.at[h, q, w], relay_send.at[h, q, w],
                     relay_recv.at[h, q, w], along(h, way, 0, c)).start()

    def send_direct(q):
        b = order[q]
        for h in range(2):
            mine = entry(h, 0, c)
            for w, way in enumerate((1, -1)):
                for core in range(2):
                    rdma(r_buf.at[h, along(h, way, b, core)], rows.at[h, q, mine], direct_send.at[h, q, w * 2 + core],
                         rows_recv.at[h, q, mine], along(h, way, 0, core)).start()
            rdma(r_buf.at[h, along(h, 0, b, 1 - c)], rows.at[h, q, mine], pair_send.at[h, q], rows_recv.at[h, q, mine],
                 partner).start()
            pltpu.make_async_copy(r_buf.at[h, along(h, 0, b, c)], rows.at[h, q, mine], local_sem.at[h, q]).start()

    def forward(q):
        for h in range(2):
            for w, way in enumerate((1, -1)):
                rdma(relay.at[h, q, w], relay.at[h, q, w], relay_send.at[h, q, w], relay_recv.at[h, q, w],
                     partner).wait_recv()
                src = entry(h, -way, c)
                rdma(relay.at[h, q, w], rows.at[h, q, src], fwd_send.at[h, q, w], rows_recv.at[h, q, src],
                     along(h, way, 0, w)).start()

    def await_rows(h, q):
        pltpu.make_async_copy(r_buf.at[h, me], rows.at[h, q, entry(h, 0, c)], local_sem.at[h, q]).wait()
        sources = [entry(h, 0, 1 - c)] + [entry(h, hops, core) for hops in (1, -1, 2) for core in range(2)]
        for src in sources:
            rdma(r_buf.at[h, me], rows.at[h, q, src], pair_send.at[h, q], rows_recv.at[h, q, src], partner).wait_recv()

    def hop1_copy(h, w):
        return rdma(part.at[h, 0, pl.ds(w * half_rows, half_rows)], hop1.at[h, w], hop1_send.at[h, w], hop1_recv.at[h, w],
                    along(h, 0, (1, -1)[w], c))

    def hop2_copy(h, w, p):
        piece = pl.ds(p * half_rows, half_rows)
        return rdma(part.at[h, 1 + w, piece], hop2.at[h, w, piece], hop2_send.at[h, w, p], hop2_recv.at[h, w, p],
                    along(h, 0, (1, -1)[w], c))

    for d, piece in first:
        send_link(d, piece)
    for piece in chip_order[:4]:
        send_chip(piece)

    for load in shared_loads:
        load.wait()
    base[...] = jnp.zeros_like(base)

    def shared_piece(j, _):
        rows_in = tok[me]
        a = jnp.dot(rows_in, w1[j], preferred_element_type=F32)
        b = jnp.dot(rows_in, w3[j], preferred_element_type=F32)
        out = jnp.dot(silu_gate(a, b), w2[j], preferred_element_type=F32)
        for h in range(2):
            base[h] += out[:, h * half_cols : (h + 1) * half_cols]
        return 0

    lax.fori_loop(0, 2, shared_piece, 0)
    for load in expert_loads:
        load.start()
    x_f32 = tok[me].astype(F32)
    logit = jnp.sum(x_f32 * sg_ref[...].astype(F32), axis=1, keepdims=True)
    for h in range(2):
        base[h] = x_f32[:, h * half_cols : (h + 1) * half_cols] + jax.nn.sigmoid(logit) * base[h]
    for load in expert_loads:
        load.wait()

    row_ids = lax.broadcasted_iota(jnp.int32, (pair, n_tok), 0)
    target = (row_ids + me * pair).astype(F32)
    n_src = 4

    def unit_device(u, i):
        dx = pick([unit[i // 2][0] + side for unit in units], u)
        dy = pick([unit[i // 2][1] + side for unit in units], u)
        col, row = lax.rem(x + dx, side), lax.rem(y + dy, side)
        return (row * side + col) * 2 + i % 2

    def out_copies(slot, srcs):
        return [pltpu.make_async_copy(
                    xe.at[slot, j, pl.ds(i * capacity, capacity), pl.ds(h * half_cols, half_cols)],
                    r_buf.at[h, srcs[i], pl.ds(j * capacity, capacity)],
                    out_sem.at[slot, (i * 2 + j) * 2 + h])
                for i in range(n_src) for j in range(2) for h in range(2)]

    n_units = len(units)

    def do_unit(u, _):
        done = 0
        for k, after in enumerate(ready):
            lo, hi = done, after
            done = after

            @pl.when(u == k)
            def _(lo=lo, hi=hi, k=k):
                for i in range(lo, hi):
                    do_step(i)
                for at in units[k]:
                    for half in range(2):
                        for p in range(2):
                            await_piece((half, at, p), 1 - c)

        slot = lax.rem(u, 2)
        srcs = [unit_device(u, i) for i in range(n_src)]
        for i in range(n_src):
            codes = meta[srcs[i], 0:8, :]
            hit = codes[0:1, :] == target
            for k in range(1, top_k):
                hit = jnp.logical_or(hit, codes[k : k + 1, :] == target)
            one_hot = jnp.where(hit, 1.0, 0.0).astype(BF16)
            picked = jnp.dot(one_hot, tok[srcs[i]], preferred_element_type=F32).astype(BF16)
            xe[slot, 0, i * capacity : (i + 1) * capacity, :] = picked[:capacity]
            xe[slot, 1, i * capacity : (i + 1) * capacity, :] = picked[capacity:]

        @pl.when(u >= 1)
        def _():
            for copy in out_copies(1 - slot, srcs):
                copy.wait()

        @pl.when(u == n_units - 3)
        def _():
            send_direct(1)
            send_direct(2)

        def do_expert(j, _):
            a = jnp.dot(xe[slot, j], w1[j], preferred_element_type=F32)
            b = jnp.dot(xe[slot, j], w3[j], preferred_element_type=F32)
            xe[slot, j] = jnp.dot(silu_gate(a, b), w2[j], preferred_element_type=F32).astype(BF16)
            return 0

        lax.fori_loop(0, 2, do_expert, 0)
        for copy in out_copies(slot, srcs):
            copy.start()
        return 0

    lax.fori_loop(0, n_units, do_unit, 0)
    for copy in out_copies((n_units - 1) % 2, [me] * n_src):
        copy.wait()
    send_relay(0)
    send_direct(0)
    send_relay(1)
    send_relay(2)

    def combine(n, _):
        q, h = n // 2, lax.rem(n, 2)

        @pl.when(n == 0)
        def _():
            forward(0)
            forward(1)
            forward(2)
            send_relay(3)

        @pl.when(n == 2)
        def _():
            send_direct(3)

        @pl.when(n == 6)
        def _():
            forward(3)
            for hh in range(2):
                for w in range(2):
                    hop1_copy(hh, w).wait_recv()
                    own = pl.ds(w * half_rows, half_rows)
                    part[hh, 1 + w, own] += hop1[hh, w]
                    hop2_copy(hh, w, w).start()

        for k in range(4):
            for hh in range(2):
                @pl.when(n == 2 * k + hh)
                def _(k=k, hh=hh):
                    await_rows(hh, k)
        b = pick([o + side for o in order], q)
        bx, by = lax.rem(x + jnp.where(h == 0, 0, b), side), lax.rem(y + jnp.where(h == 0, b, 0), side)
        dest = (by * side + bx) * 2 + c
        codes = meta[dest, 0:8, :]
        gates = meta[dest, 8:16, :]

        def weights(g, _):
            gx, gy = jnp.where(h == 0, g // 2, x), jnp.where(h == 0, y, g // 2)
            source = (gy * side + gx) * 2 + lax.rem(g, 2)
            goal = (row_ids + source * pair).astype(F32)
            w = jnp.where(codes[0:1, :] == goal, gates[0:1, :], 0.0)
            for k in range(1, top_k):
                w = jnp.where(codes[k : k + 1, :] == goal, gates[k : k + 1, :], w)
            at = pl.ds(pl.multiple_of(g * pair, pair), pair)
            hi = w.astype(BF16)
            w = w - hi.astype(F32)
            mid = w.astype(BF16)
            wt[0, at, :] = hi
            wt[1, at, :] = mid
            wt[2, at, :] = (w - mid.astype(F32)).astype(BF16)
            return 0

        lax.fori_loop(0, 2 * side, weights, 0)
        block = rows[h, q].reshape(2 * side * pair, half_cols)
        dims = (((0,), (0,)), ((), ()))
        total = lax.dot_general(wt[2], block, dims, preferred_element_type=F32)
        total += lax.dot_general(wt[1], block, dims, preferred_element_type=F32)
        total += lax.dot_general(wt[0], block, dims, preferred_element_type=F32)

        @pl.when(q < 3)
        def _():
            part[h, jnp.minimum(q, 2)] = total

        @pl.when(q == 3)
        def _():
            base[h] += total

        for hh in range(2):
            @pl.when(n == hh)
            def _(hh=hh):
                for w in range(2):
                    hop1_copy(hh, w).start()
            for w in range(2):
                @pl.when(n == 2 * (1 + w) + hh)
                def _(hh=hh, w=w):
                    hop2_copy(hh, w, 1 - w).start()
        return 0

    lax.fori_loop(0, 8, combine, 0)
    for h in range(2):
        for w in range(2):
            for p in range(2):
                hop2_copy(h, w, p).wait_recv()
        y_out[:, h * half_cols : (h + 1) * half_cols] = (base[h] + (hop2[h, 0] + hop2[h, 1])).astype(BF16)

    for d in range(4):
        for i, piece in enumerate(link_order[d]):
            piece_copy(piece, me, link_send.at[d, i], partner).wait_send()
        for i in range(len(meta_order[d])):
            meta_copy(me, meta_link_send.at[d, i], partner).wait_send()
    for i, piece in enumerate(chip_order):
        piece_copy(piece, me, chip_send.at[i], partner).wait_send()
    for i in range(len(meta_chip_order)):
        meta_copy(me, meta_chip_send.at[i], partner).wait_send()
    for h in range(2):
        for q in range(4):
            sems = [relay_send.at[h, q, w] for w in range(2)] + [fwd_send.at[h, q, w] for w in range(2)]
            sems += [direct_send.at[h, q, k] for k in range(4)] + [pair_send.at[h, q]]
            for sem in sems:
                rdma(r_buf.at[h, me], rows.at[h, q, 0], sem, rows_recv.at[h, q, 0], partner).wait_send()
        for w in range(2):
            hop1_copy(h, w).wait_send()
            for p in range(2):
                hop2_copy(h, w, p).wait_send()


def solution(mesh):
    num_ep = mesh.shape['ep']
    side = math.isqrt(num_ep // 2)
    assert side == 4 and 2 * side * side == num_ep
    row_spec = P(('dp', 'ep'), None)
    replicated = P()
    expert_spec = P('ep', None, None)
    vmem, anywhere = pl.BlockSpec(memory_space=pltpu.VMEM), pl.BlockSpec(memory_space=pl.ANY)
    dma = pltpu.SemaphoreType.DMA

    def device_step(tokens, expert_ids, gate_vals, slots, shared_w1, shared_w3, shared_w2, shared_gate, expert_w1, expert_w3, expert_w2):
        tok_count, hidden = tokens.shape
        top_k = expert_ids.shape[1]
        local_experts, _, ff = expert_w1.shape
        num_experts = local_experts * num_ep
        capacity = 8 * ((2 * tok_count * top_k + 8 * num_experts - 1) // (8 * num_experts))
        assert local_experts == 2 and top_k < 8 and capacity % 16 == 0 and shared_w1.shape[1] == 2 * ff
        pair = local_experts * capacity
        half = hidden // 2
        y, _, _ = pl.pallas_call(
            functools.partial(layer_kernel, side, capacity),
            out_shape=(jax.ShapeDtypeStruct((tok_count, hidden), BF16),
                       jax.ShapeDtypeStruct((2, num_ep, pair, half), BF16),
                       jax.ShapeDtypeStruct((2, 4, 2, pair, half), BF16)),
            in_specs=[anywhere] + [vmem] * 3 + [anywhere] * 3 + [vmem] + [anywhere] * 3,
            out_specs=(vmem, anywhere, anywhere),
            scratch_shapes=[
                pltpu.VMEM((num_ep, tok_count, hidden), BF16),
                pltpu.VMEM((num_ep, 16, tok_count), F32),
                pltpu.VMEM((2, tok_count, half), F32),
                pltpu.VMEM((local_experts, hidden, ff), BF16),
                pltpu.VMEM((local_experts, hidden, ff), BF16),
                pltpu.VMEM((local_experts, ff, hidden), BF16),
                pltpu.VMEM((2, local_experts, 4 * capacity, hidden), BF16),
                pltpu.VMEM((2, 4, 2 * side, pair, half), BF16),
                pltpu.VMEM((3, 2 * side * pair, tok_count), BF16),
                pltpu.VMEM((2, 3, tok_count, half), F32),
                pltpu.VMEM((2, 2, tok_count // 2, half), F32),
                pltpu.VMEM((2, 2, tok_count, half), F32),
                dma((10,)), dma((4, 15)), dma((64,)), dma((num_ep, 4)), dma((4, 15)), dma((16,)), dma((num_ep,)),
                dma((2, 16)),
                dma((2, 4, 4)), dma((2, 4, 2)), dma((2, 4, 2)), dma((2, 4)), dma((2, 4)), dma((2, 4, 2 * side)),
                dma((2, 4, 2)), dma((2, 2)), dma((2, 2)), dma((2, 2, 2)), dma((2, 2, 2)),
            ],
            compiler_params=pltpu.CompilerParams(collective_id=0, has_side_effects=True, vmem_limit_bytes=VMEM_LIMIT),
            name='moe_layer',
        )(tokens, expert_ids.T, slots.T, gate_vals.T, shared_w1, shared_w3, shared_w2, shared_gate.reshape(1, hidden),
          expert_w1, expert_w3, expert_w2)
        return y

    return jax.shard_map(device_step, mesh=mesh, in_specs=(row_spec, row_spec, row_spec, row_spec, replicated, replicated, replicated, replicated, expert_spec, expert_spec, expert_spec), out_specs=row_spec, check_vma=False)
```

time: 198 us -> 162 us (0.82)
  Pallas kernels: 192 us -> 159 us
  other arithmetic: 2.03 us -> 0 us
    pallas_call x2 -> x1, Pallas kernels: 192 us -> 159 us  [device_step(): pl.pallas_call(functools.partial(layer_kernel, side, capacity), out_shape...]
where the time goes in v2:
time: 162 us
  Pallas kernels  159 us (98%)
  local copies, waits for them, and re-layouts  3.35 us (2%)
    pallas_call x1, Pallas kernels, device_step(): pl.pallas_call(functools.partial(layer_kernel, side, capacity), out_shape...  159 us

profile of v2, /device:TPU:97, one launch (start us, length us, event | category | flops | bytes accessed | tf_op | source)
XLA Modules:
  0.0 162.1 jit_solution(5295442174288620266)
XLA Ops:
  0.0 1.3 reshape.3.sg_ref
  1.3 158.8 %moe_layer.1 = (bf16[256,1536]{1,0:T(8,128)(2,1)}, bf16[2,32,96,768]{3,2,1,0:T(8,128)(2,1)}, bf16[2,4,2,96,768]{4,3,2,1,0:T(8,128)(2,1)}) custom-call(bf16[256,1536]{1,0:T(8,128)(2,1)} %tok_in.1, s32[6,256]{1,0:T(8,128)} %bitcast.3, s32[6,256]{1,0:T(8,128)} %bitcast.4, f32[6,256]{1,0:T(8,128)} %bitcast.5, bf16[1536,1024]{1,0:T(8,128)(2,1)} %sw1_in.1, ...), custom_call_target="tpu_custom_call" | custom-call | tf_op jit(solution)/shard_map/moe_layer/pallas_call | solution.py:470
  160.1 2.1 %copy.13 = bf16[256,1536]{1,0:T(8,128)(2,1)} copy(bf16[256,1536]{1,0:T(8,128)(2,1)} %get-tuple-element.6) | data formatting | bytes 1572864

commit v3 on v2

--- a/solution.py
+++ b/solution.py
@@ -94,21 +94,12 @@
 def layer_kernel(side, capacity, tok_in, ids_ref, slots_ref, gates_ref, sw1_in, sw3_in, sw2_in, sg_ref, w1_in, w3_in, w2_in,
                  y_out, r_buf, relay,
                  tok, meta, base, w1, w3, w2, xe, rows, wt, part, hop1, hop2,
-                 load_sem, link_send, chip_send, recv, meta_link_send, meta_chip_send, meta_recv, out_sem,
-                 direct_send, relay_send, fwd_send, pair_send, local_sem, rows_recv, relay_recv,
-                 hop1_send, hop1_recv, hop2_send, hop2_recv):
+                 load_sem, link_send, chip_send, meta_send, link_recv, chip_recv, meta_link_recv, meta_chip_recv, out_sem,
+                 direct_send, relay_send, rows_recv, relay_recv, hop1_send, hop1_recv, hop2_send, hop2_recv):
     me, x, y, c = place(side)
     first, steps = plan_gather()
     units, ready = plan_units(steps)
-    link_order = [[piece for e, piece in first if e == d] for d in range(4)]
-    chip_order = [(half, (0, 0), p) for half in range(2) for p in range(2)]
-    for arrivals in steps:
-        for _, piece, onward in arrivals:
-            chip_order.append(piece)
-            for e in onward:
-                link_order[e].append(piece)
-    meta_order = [[piece for piece in link_order[d] if carries_meta(piece)] for d in range(4)]
-    meta_chip_order = [piece for piece in chip_order if carries_meta(piece)]
+    n_steps = len(steps)
     top_k = ids_ref.shape[0]
     n_tok, hidden = tok_in.shape
     half_cols, half_rows = hidden // 2, n_tok // 2
@@ -139,11 +130,11 @@
     shared_loads, expert_loads = [], []
     for j in range(2):
         cols = pl.ds(j * ff, ff)
-        shared_loads += [pltpu.make_async_copy(sw1_in.at[:, cols], w1.at[j], load_sem.at[1 + j]),
-                         pltpu.make_async_copy(sw3_in.at[:, cols], w3.at[j], load_sem.at[3 + j]),
-                         pltpu.make_async_copy(sw2_in.at[cols], w2.at[j], load_sem.at[5 + j])]
+        shared_loads += [pltpu.make_async_copy(sw1_in.at[:, cols], w1.at[j], load_sem.at[1]),
+                         pltpu.make_async_copy(sw3_in.at[:, cols], w3.at[j], load_sem.at[2]),
+                         pltpu.make_async_copy(sw2_in.at[cols], w2.at[j], load_sem.at[3])]
     for k, (src, dst) in enumerate(((w1_in, w1), (w3_in, w3), (w2_in, w2))):
-        expert_loads.append(pltpu.make_async_copy(src, dst, load_sem.at[7 + k]))
+        expert_loads.append(pltpu.make_async_copy(src, dst, load_sem.at[1 + k]))
     for load in shared_loads:
         load.start()
 
@@ -161,37 +152,46 @@
     def view(half, src, p):
         return tok.at[src, pl.ds(p * half_rows, half_rows), pl.ds(half * half_cols, half_cols)]
 
-    def piece_copy(piece, src, send, to):
-        half, _, p = piece
-        return rdma(view(half, src, p), view(half, src, p), send, recv.at[src, half * 2 + p], to)
-
-    def meta_copy(src, send, to):
-        return rdma(meta.at[src], meta.at[src], send, meta_recv.at[src], to)
+    sent_at = {}
+    for i, arrivals in enumerate(steps):
+        for d, (half, at, p), _ in arrivals:
+            sent_at[d, half, shift(DIRS[d][0], -DIRS[d][1], at), p] = i
 
     def send_link(d, piece):
-        src = device(piece[1])
-        piece_copy(piece, src, link_send.at[d, link_order[d].index(piece)], neighbour(d)).start()
+        half, at, p = piece
+        src, i = device(at), sent_at[d, half, at, p]
+        rdma(view(half, src, p), view(half, src, p), link_send.at[0], link_recv.at[i], neighbour(d)).start()
         if carries_meta(piece):
-            meta_copy(src, meta_link_send.at[d, meta_order[d].index(piece)], neighbour(d)).start()
-
-    def send_chip(piece):
-        src = device(piece[1])
-        piece_copy(piece, src, chip_send.at[chip_order.index(piece)], partner).start()
+            rdma(meta.at[src], meta.at[src], meta_send.at[0], meta_link_recv.at[i], neighbour(d)).start()
+
+    def send_chip(i, piece):
+        half, at, p = piece
+        src = device(at)
+        rdma(view(half, src, p), view(half, src, p), chip_send.at[0], chip_recv.at[i], partner).start()
         if carries_meta(piece):
-            meta_copy(src, meta_chip_send.at[meta_chip_order.index(piece)], partner).start()
-
-    def await_piece(piece, core):
-        src = device(piece[1], core)
-        piece_copy(piece, src, link_send.at[0, 0], partner).wait_recv()
-        if carries_meta(piece):
-            meta_copy(src, meta_link_send.at[0, 0], partner).wait_recv()
+            rdma(meta.at[src], meta.at[src], meta_send.at[0], meta_chip_recv.at[i], partner).start()
+
+    own_pieces = [(half, (0, 0), p) for half in range(2) for p in range(2)]
+
+    def await_bytes(sem, ref):
+        rdma(ref, ref, sem, sem, partner).wait_recv()
+
+    def await_pieces(pieces, sem, meta_sem):
+        await_bytes(sem, tok.at[0])
+        n = sum(carries_meta(piece) for piece in pieces)
+        if n:
+            await_bytes(meta_sem, meta.at[pl.ds(0, n)])
 
     def do_step(i):
+        await_pieces([piece for _, piece, _ in steps[i]], link_recv.at[i], meta_link_recv.at[i])
         for d, piece, onward in steps[i]:
-            await_piece(piece, None)
             for e in onward:
                 send_link(e, piece)
-            send_chip(piece)
+            send_chip(i + 1, piece)
+
+    def await_chip_step(i):
+        pieces = own_pieces if i == 0 else [piece for _, piece, _ in steps[i - 1]]
+        await_pieces(pieces, chip_recv.at[i], meta_chip_recv.at[i])
 
     order = (2, 1, -1, 0)
 
@@ -201,8 +201,8 @@
     def send_relay(q):
         for h in range(2):
             for w, way in enumerate((1, -1)):
-                rdma(r_buf.at[h, along(h, 2, order[q], w)], relay.at[h, q, w], relay_send.at[h, q, w],
-                     relay_recv.at[h, q, w], along(h, way, 0, c)).start()
+                rdma(r_buf.at[h, along(h, 2, order[q], w)], relay.at[q, h, w], relay_send.at[0],
+                     relay_recv.at[q], along(h, way, 0, c)).start()
 
     def send_direct(q):
         b = order[q]
@@ -210,42 +210,37 @@
             mine = entry(h, 0, c)
             for w, way in enumerate((1, -1)):
                 for core in range(2):
-                    rdma(r_buf.at[h, along(h, way, b, core)], rows.at[h, q, mine], direct_send.at[h, q, w * 2 + core],
-                         rows_recv.at[h, q, mine], along(h, way, 0, core)).start()
-            rdma(r_buf.at[h, along(h, 0, b, 1 - c)], rows.at[h, q, mine], pair_send.at[h, q], rows_recv.at[h, q, mine],
+                    rdma(r_buf.at[h, along(h, way, b, core)], rows.at[h, q, mine], direct_send.at[0],
+                         rows_recv.at[h, q], along(h, way, 0, core)).start()
+            rdma(r_buf.at[h, along(h, 0, b, 1 - c)], rows.at[h, q, mine], direct_send.at[0], rows_recv.at[h, q],
                  partner).start()
-            pltpu.make_async_copy(r_buf.at[h, along(h, 0, b, c)], rows.at[h, q, mine], local_sem.at[h, q]).start()
+            pltpu.make_async_copy(r_buf.at[h, along(h, 0, b, c)], rows.at[h, q, mine], rows_recv.at[h, q]).start()
 
     def forward(q):
+        await_bytes(relay_recv.at[q], relay.at[q])
         for h in range(2):
             for w, way in enumerate((1, -1)):
-                rdma(relay.at[h, q, w], relay.at[h, q, w], relay_send.at[h, q, w], relay_recv.at[h, q, w],
-                     partner).wait_recv()
-                src = entry(h, -way, c)
-                rdma(relay.at[h, q, w], rows.at[h, q, src], fwd_send.at[h, q, w], rows_recv.at[h, q, src],
+                rdma(relay.at[q, h, w], rows.at[h, q, entry(h, -way, c)], relay_send.at[0], rows_recv.at[h, q],
                      along(h, way, 0, w)).start()
 
     def await_rows(h, q):
-        pltpu.make_async_copy(r_buf.at[h, me], rows.at[h, q, entry(h, 0, c)], local_sem.at[h, q]).wait()
-        sources = [entry(h, 0, 1 - c)] + [entry(h, hops, core) for hops in (1, -1, 2) for core in range(2)]
-        for src in sources:
-            rdma(r_buf.at[h, me], rows.at[h, q, src], pair_send.at[h, q], rows_recv.at[h, q, src], partner).wait_recv()
+        await_bytes(rows_recv.at[h, q], rows.at[h, q])
 
     def hop1_copy(h, w):
-        return rdma(part.at[h, 0, pl.ds(w * half_rows, half_rows)], hop1.at[h, w], hop1_send.at[h, w], hop1_recv.at[h, w],
+        return rdma(part.at[h, 0, pl.ds(w * half_rows, half_rows)], hop1.at[h, w], hop1_send.at[0], hop1_recv.at[0],
                     along(h, 0, (1, -1)[w], c))
 
     def hop2_copy(h, w, p):
         piece = pl.ds(p * half_rows, half_rows)
-        return rdma(part.at[h, 1 + w, piece], hop2.at[h, w, piece], hop2_send.at[h, w, p], hop2_recv.at[h, w, p],
+        return rdma(part.at[h, 1 + w, piece], hop2.at[h, w, piece], hop2_send.at[0], hop2_recv.at[0],
                     along(h, 0, (1, -1)[w], c))
 
     for d, piece in first:
         send_link(d, piece)
-    for piece in chip_order[:4]:
-        send_chip(piece)
-
-    for load in shared_loads:
+    for piece in own_pieces:
+        send_chip(0, piece)
+
+    for load in expert_loads:
         load.wait()
     base[...] = jnp.zeros_like(base)
 
@@ -262,7 +257,7 @@
     for load in expert_loads:
         load.start()
     x_f32 = tok[me].astype(F32)
-    logit = jnp.sum(x_f32 * sg_ref[...].astype(F32), axis=1, keepdims=True)
+    logit = jnp.sum(x_f32 * sg_ref[...].astype(F32).reshape(1, hidden), axis=1, keepdims=True)
     for h in range(2):
         base[h] = x_f32[:, h * half_cols : (h + 1) * half_cols] + jax.nn.sigmoid(logit) * base[h]
     for load in expert_loads:
@@ -282,8 +277,11 @@
         return [pltpu.make_async_copy(
                     xe.at[slot, j, pl.ds(i * capacity, capacity), pl.ds(h * half_cols, half_cols)],
                     r_buf.at[h, srcs[i], pl.ds(j * capacity, capacity)],
-                    out_sem.at[slot, (i * 2 + j) * 2 + h])
+                    out_sem.at[slot])
                 for i in range(n_src) for j in range(2) for h in range(2)]
+
+    def await_out(slot):
+        pltpu.make_async_copy(r_buf.at[0, pl.ds(0, 2 * side)], rows.at[0, 0], out_sem.at[slot]).wait()
 
     n_units = len(units)
 
@@ -297,10 +295,8 @@
             def _(lo=lo, hi=hi, k=k):
                 for i in range(lo, hi):
                     do_step(i)
-                for at in units[k]:
-                    for half in range(2):
-                        for p in range(2):
-                            await_piece((half, at, p), 1 - c)
+                for i in range(lo + 1 if lo else 0, hi + 1):
+                    await_chip_step(i)
 
         slot = lax.rem(u, 2)
         srcs = [unit_device(u, i) for i in range(n_src)]
@@ -316,8 +312,7 @@
 
         @pl.when(u >= 1)
         def _():
-            for copy in out_copies(1 - slot, srcs):
-                copy.wait()
+            await_out(1 - slot)
 
         @pl.when(u == n_units - 3)
         def _():
@@ -336,8 +331,7 @@
         return 0
 
     lax.fori_loop(0, n_units, do_unit, 0)
-    for copy in out_copies((n_units - 1) % 2, [me] * n_src):
-        copy.wait()
+    await_out((n_units - 1) % 2)
     send_relay(0)
     send_direct(0)
     send_relay(1)
@@ -360,9 +354,9 @@
         @pl.when(n == 6)
         def _():
             forward(3)
+            await_bytes(hop1_recv.at[0], hop1)
             for hh in range(2):
                 for w in range(2):
-                    hop1_copy(hh, w).wait_recv()
                     own = pl.ds(w * half_rows, half_rows)
                     part[hh, 1 + w, own] += hop1[hh, w]
                     hop2_copy(hh, w, w).start()
@@ -421,31 +415,20 @@
         return 0
 
     lax.fori_loop(0, 8, combine, 0)
+    await_bytes(hop2_recv.at[0], hop2)
     for h in range(2):
-        for w in range(2):
-            for p in range(2):
-                hop2_copy(h, w, p).wait_recv()
         y_out[:, h * half_cols : (h + 1) * half_cols] = (base[h] + (hop2[h, 0] + hop2[h, 1])).astype(BF16)
 
-    for d in range(4):
-        for i, piece in enumerate(link_order[d]):
-            piece_copy(piece, me, link_send.at[d, i], partner).wait_send()
-        for i in range(len(meta_order[d])):
-            meta_copy(me, meta_link_send.at[d, i], partner).wait_send()
-    for i, piece in enumerate(chip_order):
-        piece_copy(piece, me, chip_send.at[i], partner).wait_send()
-    for i in range(len(meta_chip_order)):
-        meta_copy(me, meta_chip_send.at[i], partner).wait_send()
-    for h in range(2):
-        for q in range(4):
-            sems = [relay_send.at[h, q, w] for w in range(2)] + [fwd_send.at[h, q, w] for w in range(2)]
-            sems += [direct_send.at[h, q, k] for k in range(4)] + [pair_send.at[h, q]]
-            for sem in sems:
-                rdma(r_buf.at[h, me], rows.at[h, q, 0], sem, rows_recv.at[h, q, 0], partner).wait_send()
-        for w in range(2):
-            hop1_copy(h, w).wait_send()
-            for p in range(2):
-                hop2_copy(h, w, p).wait_send()
+    def await_sent(sem, ref):
+        rdma(ref, ref, sem, sem, partner).wait_send()
+
+    await_sent(link_send.at[0], tok.at[pl.ds(0, n_steps)])
+    await_sent(chip_send.at[0], tok.at[pl.ds(0, n_steps + 1)])
+    await_sent(meta_send.at[0], meta.at[pl.ds(0, 2 * n_steps + 1)])
+    await_sent(direct_send.at[0], r_buf.at[:, pl.ds(0, 20)])
+    await_sent(relay_send.at[0], r_buf.at[:, pl.ds(0, 16)])
+    await_sent(hop1_send.at[0], hop1)
+    await_sent(hop2_send.at[0], hop2)
 
 
 def solution(mesh):
@@ -471,7 +454,7 @@
             functools.partial(layer_kernel, side, capacity),
             out_shape=(jax.ShapeDtypeStruct((tok_count, hidden), BF16),
                        jax.ShapeDtypeStruct((2, num_ep, pair, half), BF16),
-                       jax.ShapeDtypeStruct((2, 4, 2, pair, half), BF16)),
+                       jax.ShapeDtypeStruct((4, 2, 2, pair, half), BF16)),
             in_specs=[anywhere] + [vmem] * 3 + [anywhere] * 3 + [vmem] + [anywhere] * 3,
             out_specs=(vmem, anywhere, anywhere),
             scratch_shapes=[
@@ -487,14 +470,12 @@
                 pltpu.VMEM((2, 3, tok_count, half), F32),
                 pltpu.VMEM((2, 2, tok_count // 2, half), F32),
                 pltpu.VMEM((2, 2, tok_count, half), F32),
-                dma((10,)), dma((4, 15)), dma((64,)), dma((num_ep, 4)), dma((4, 15)), dma((16,)), dma((num_ep,)),
-                dma((2, 16)),
-                dma((2, 4, 4)), dma((2, 4, 2)), dma((2, 4, 2)), dma((2, 4)), dma((2, 4)), dma((2, 4, 2 * side)),
-                dma((2, 4, 2)), dma((2, 2)), dma((2, 2)), dma((2, 2, 2)), dma((2, 2, 2)),
+                dma((4,)), dma((1,)), dma((1,)), dma((1,)), dma((15,)), dma((16,)), dma((15,)), dma((16,)), dma((2,)),
+                dma((1,)), dma((1,)), dma((2, 4)), dma((4,)), dma((1,)), dma((1,)), dma((1,)), dma((1,)),
             ],
             compiler_params=pltpu.CompilerParams(collective_id=0, has_side_effects=True, vmem_limit_bytes=VMEM_LIMIT),
             name='moe_layer',
-        )(tokens, expert_ids.T, slots.T, gate_vals.T, shared_w1, shared_w3, shared_w2, shared_gate.reshape(1, hidden),
+        )(tokens, expert_ids.T, slots.T, gate_vals.T, shared_w1, shared_w3, shared_w2, shared_gate,
           expert_w1, expert_w3, expert_w2)
         return y
 

time: 162 us -> 156 us (0.963)
  Pallas kernels: 159 us -> 154 us
    pallas_call x1, Pallas kernels: 159 us -> 154 us  [device_step(): pl.pallas_call(functools.partial(layer_kernel, side, capacity), out_shape...]
where the time goes in v3:
time: 156 us
  Pallas kernels  154 us (99%)
  local copies, waits for them, and re-layouts  2.06 us (1%)
    pallas_call x1, Pallas kernels, device_step(): pl.pallas_call(functools.partial(layer_kernel, side, capacity), out_shape...  154 us

profile of v3, /device:TPU:97, one launch (start us, length us, event | category | flops | bytes accessed | tf_op | source)
XLA Modules:
  0.0 156.0 jit_solution(9324546890080439515)
XLA Ops:
  0.0 153.9 %moe_layer.1 = (bf16[256,1536]{1,0:T(8,128)(2,1)}, bf16[2,32,96,768]{3,2,1,0:T(8,128)(2,1)}, bf16[4,2,2,96,768]{4,3,2,1,0:T(8,128)(2,1)}) custom-call(bf16[256,1536]{1,0:T(8,128)(2,1)} %tok_in.1, s32[6,256]{1,0:T(8,128)} %bitcast.3, s32[6,256]{1,0:T(8,128)} %bitcast.4, f32[6,256]{1,0:T(8,128)} %bitcast.5, bf16[1536,1024]{1,0:T(8,128)(2,1)} %sw1_in.1, ...), custom_call_target="tpu_custom_call" | custom-call | tf_op jit(solution)/shard_map/moe_layer/pallas_call | solution.py:453
  153.9 2.1 %copy.13 = bf16[256,1536]{1,0:T(8,128)(2,1)} copy(bf16[256,1536]{1,0:T(8,128)(2,1)} %get-tuple-element.6) | data formatting | bytes 1572864

commit v4 on v3

--- a/solution.py
+++ b/solution.py
@@ -25,53 +25,46 @@
     return tuple(moved)
 
 
-def ahead_piece(way):
-    return 0 if way > 0 else 1
-
-
 def plan_gather():
-    queues = [[] for _ in DIRS]
-    first = []
-    for d, (axis, way) in enumerate(DIRS):
-        for half in (axis, 1 - axis):
-            for p in (ahead_piece(way), 1 - ahead_piece(way)):
-                queues[d].append((half, (0, 0), p))
-                first.append((d, (half, (0, 0), p)))
-    steps = []
-    while any(queues):
-        moved = [q.pop(0) if q else None for q in queues]
-        arrivals = []
-        for d, piece in enumerate(moved):
-            if piece is None:
-                continue
-            half, at, p = piece
-            axis, way = DIRS[d]
-            at = shift(axis, way, at)
-            onward = []
-            if p == ahead_piece(way) and abs(at[axis]) == 1:
-                onward.append(d)
-            if axis == half:
-                onward += [e for e, (other, _) in enumerate(DIRS) if other != axis]
-            for e in onward:
-                queues[e].append((half, at, p))
-            arrivals.append((d, (half, at, p), onward))
-        steps.append(arrivals)
-    return first, steps
-
-
-def plan_units(steps, chips_per_unit=2):
+    slots = []
+    for kind, g in (('F1w', 0), ('F1a', 0), ('F2', 0), ('Ga', 0), ('F1f', 0), ('F2', -1), ('F2', 1), ('F2', 2), ('Ga', -1),
+                    ('Ga', 1), ('Ga', 2), ('Gb', 0), ('Gb', -1), ('Gb', 1), ('Gb', 2)):
+        messages = []
+        for d, (a, v) in enumerate(DIRS):
+            at = [0, 0]
+            quarter = (a, v) if kind in ('F1w', 'F1f') else (a, -v) if kind == 'F1a' else (1 - a, -v if kind == 'Ga' else v)
+            if kind in ('F1f', 'Gb'):
+                at[a] = -v
+            if kind in ('F2', 'Ga', 'Gb'):
+                at[1 - a] = wrap(g * quarter[1])
+            messages.append((d, quarter, tuple(at)))
+        slots.append((kind[0] == 'F', messages))
+    sends = {-1: (0, 1, 2, 3), 0: (4, 5), 1: (6,), 4: (7, 8, 9), 5: (10, 11), 9: (12, 13), 10: (14,)}
+    return slots, sends
+
+
+def plan_units(slots, chips_per_unit=2):
     done = {(0, 0): 0}
-    for i, arrivals in enumerate(steps):
-        for _, (_, at, _), _ in arrivals:
-            done[at] = i + 1
+    for i, (_, messages) in enumerate(slots):
+        for d, _, at in messages:
+            done[shift(*DIRS[d], at)] = i + 1
     order = sorted(done, key=lambda at: (done[at], at))
     units = [order[i : i + chips_per_unit] for i in range(0, len(order), chips_per_unit)]
     return units, [max(done[at] for at in unit) for unit in units]
 
 
-def carries_meta(piece):
-    half, _, p = piece
-    return half == 0 and p == 0
+def is_whole(quarter, at):
+    h, w = quarter
+    return at[1 - h] in (0, -w)
+
+
+def carries_meta(quarter, at):
+    h, w = quarter
+    if w != 1 or at[h] == 0:
+        return False
+    if at[1 - h] == 0:
+        return True
+    return h == (1 if abs(at[0]) == 1 and at[1] == 2 else 0)
 
 
 def place(side):
@@ -93,16 +86,17 @@
 
 def layer_kernel(side, capacity, tok_in, ids_ref, slots_ref, gates_ref, sw1_in, sw3_in, sw2_in, sg_ref, w1_in, w3_in, w2_in,
                  y_out, r_buf, relay,
-                 tok, meta, base, w1, w3, w2, xe, rows, wt, part, hop1, hop2,
-                 load_sem, link_send, chip_send, meta_send, link_recv, chip_recv, meta_link_recv, meta_chip_recv, out_sem,
+                 tok, picked_rows, meta, base, w1, w3, w2, xe, rows, wt, part, hop1, hop2,
+                 load_sem, link_send, pick_send, chip_send, meta_send, link_recv, chip_recv, meta_link_recv, meta_chip_recv, out_sem,
                  direct_send, relay_send, rows_recv, relay_recv, hop1_send, hop1_recv, hop2_send, hop2_recv):
     me, x, y, c = place(side)
-    first, steps = plan_gather()
-    units, ready = plan_units(steps)
-    n_steps = len(steps)
+    slots, sends = plan_gather()
+    units, ready = plan_units(slots)
+    quarters = [(h, w) for h in range(2) for w in (1, -1)]
     top_k = ids_ref.shape[0]
     n_tok, hidden = tok_in.shape
     half_cols, half_rows = hidden // 2, n_tok // 2
+    quarter_cols = hidden // 4
     ff = w1.shape[2]
     pair = 2 * capacity
     here = (x, y)
@@ -149,49 +143,83 @@
     tok_load.wait()
     pl.semaphore_wait(barrier, 9)
 
-    def view(half, src, p):
-        return tok.at[src, pl.ds(p * half_rows, half_rows), pl.ds(half * half_cols, half_cols)]
-
-    sent_at = {}
-    for i, arrivals in enumerate(steps):
-        for d, (half, at, p), _ in arrivals:
-            sent_at[d, half, shift(DIRS[d][0], -DIRS[d][1], at), p] = i
-
-    def send_link(d, piece):
-        half, at, p = piece
-        src, i = device(at), sent_at[d, half, at, p]
-        rdma(view(half, src, p), view(half, src, p), link_send.at[0], link_recv.at[i], neighbour(d)).start()
-        if carries_meta(piece):
-            rdma(meta.at[src], meta.at[src], meta_send.at[0], meta_link_recv.at[i], neighbour(d)).start()
-
-    def send_chip(i, piece):
-        half, at, p = piece
-        src = device(at)
-        rdma(view(half, src, p), view(half, src, p), chip_send.at[0], chip_recv.at[i], partner).start()
-        if carries_meta(piece):
-            rdma(meta.at[src], meta.at[src], meta_send.at[0], meta_chip_recv.at[i], partner).start()
-
-    own_pieces = [(half, (0, 0), p) for half in range(2) for p in range(2)]
+    def columns(quarter):
+        return pl.ds(quarters.index(quarter) * quarter_cols, quarter_cols)
+
+    def view(quarter, src):
+        return tok.at[src, :, columns(quarter)]
+
+    def one_hot_rows(codes, goal):
+        hit = codes[0:1, :] == goal
+        for k in range(1, top_k):
+            hit = jnp.logical_or(hit, codes[k : k + 1, :] == goal)
+        return jnp.where(hit, 1.0, 0.0).astype(BF16)
+
+    chip_ids = lax.broadcasted_iota(jnp.int32, (2 * pair, n_tok), 0)
+    picks = [i for i, (whole, _) in enumerate(slots) if not whole]
+    group_of = {i: k % 5 for k, i in enumerate(picks)}
+
+    def await_sent(sem, ref):
+        rdma(ref, ref, sem, sem, partner).wait_send()
+
+    def await_picks_sent(group):
+        await_sent(pick_send.at[group], tok.at[0, pl.ds(0, 2 * pair)])
+
+    def send_slot(i):
+        whole, messages = slots[i]
+        if not whole:
+            if picks.index(i) >= 5:
+                await_picks_sent(group_of[i])
+            for d, quarter, at in messages:
+                src = device(at)
+                goal = (chip_ids + neighbour(d, 0) * pair).astype(F32)
+                one_hot = one_hot_rows(meta[src, 0:8, :], goal)
+                picked = jnp.dot(one_hot, tok[src, :, columns(quarter)], preferred_element_type=F32)
+                picked_rows[group_of[i], d] = picked.astype(BF16)
+        for d, quarter, at in messages:
+            src = device(at)
+            if whole:
+                rdma(view(quarter, src), view(quarter, src), link_send.at[0], link_recv.at[i], neighbour(d)).start()
+            else:
+                for core in range(2):
+                    rdma(picked_rows.at[group_of[i], d, pl.ds(core * pair, pair)],
+                         tok.at[src, pl.ds(0, pair), columns(quarter)], pick_send.at[group_of[i]], link_recv.at[i], neighbour(d, core)).start()
+            if carries_meta(quarter, shift(*DIRS[d], at)):
+                for core in (None,) if whole else (0, 1):
+                    rdma(meta.at[src], meta.at[src], meta_send.at[0], meta_link_recv.at[i], neighbour(d, core)).start()
 
     def await_bytes(sem, ref):
         rdma(ref, ref, sem, sem, partner).wait_recv()
 
-    def await_pieces(pieces, sem, meta_sem):
-        await_bytes(sem, tok.at[0])
-        n = sum(carries_meta(piece) for piece in pieces)
+    def metas(i):
+        return sum(carries_meta(quarter, shift(*DIRS[d], at)) for d, quarter, at in slots[i][1])
+
+    def await_slot(i):
+        whole, messages = slots[i]
+        await_bytes(link_recv.at[i], tok.at[0] if whole else tok.at[0, pl.ds(0, 2 * pair)])
+        if metas(i):
+            await_bytes(meta_link_recv.at[i], meta.at[pl.ds(0, metas(i) * (1 if whole else 2))])
+
+    def do_slot(i):
+        await_slot(i)
+        whole, messages = slots[i]
+        if whole:
+            for d, quarter, at in messages:
+                at = shift(*DIRS[d], at)
+                src = device(at)
+                rdma(view(quarter, src), view(quarter, src), chip_send.at[0], chip_recv.at[i + 1], partner).start()
+                if carries_meta(quarter, at):
+                    rdma(meta.at[src], meta.at[src], meta_send.at[0], meta_chip_recv.at[i + 1], partner).start()
+        for j in sends.get(i, ()):
+            send_slot(j)
+
+    def await_chip_slot(i):
+        if i and not slots[i - 1][0]:
+            return
+        await_bytes(chip_recv.at[i], tok.at[0])
+        n = metas(i - 1) if i else 1
         if n:
-            await_bytes(meta_sem, meta.at[pl.ds(0, n)])
-
-    def do_step(i):
-        await_pieces([piece for _, piece, _ in steps[i]], link_recv.at[i], meta_link_recv.at[i])
-        for d, piece, onward in steps[i]:
-            for e in onward:
-                send_link(e, piece)
-            send_chip(i + 1, piece)
-
-    def await_chip_step(i):
-        pieces = own_pieces if i == 0 else [piece for _, piece, _ in steps[i - 1]]
-        await_pieces(pieces, chip_recv.at[i], meta_chip_recv.at[i])
+            await_bytes(meta_chip_recv.at[i], meta.at[pl.ds(0, n)])
 
     order = (2, 1, -1, 0)
 
@@ -235,10 +263,10 @@
         return rdma(part.at[h, 1 + w, piece], hop2.at[h, w, piece], hop2_send.at[0], hop2_recv.at[0],
                     along(h, 0, (1, -1)[w], c))
 
-    for d, piece in first:
-        send_link(d, piece)
-    for piece in own_pieces:
-        send_chip(0, piece)
+    for j in sends[-1]:
+        send_slot(j)
+    rdma(tok.at[me], tok.at[me], chip_send.at[0], chip_recv.at[0], partner).start()
+    rdma(meta.at[me], meta.at[me], meta_send.at[0], meta_chip_recv.at[0], partner).start()
 
     for load in expert_loads:
         load.wait()
@@ -294,21 +322,28 @@
             @pl.when(u == k)
             def _(lo=lo, hi=hi, k=k):
                 for i in range(lo, hi):
-                    do_step(i)
+                    do_slot(i)
                 for i in range(lo + 1 if lo else 0, hi + 1):
-                    await_chip_step(i)
+                    await_chip_slot(i)
 
         slot = lax.rem(u, 2)
         srcs = [unit_device(u, i) for i in range(n_src)]
         for i in range(n_src):
-            codes = meta[srcs[i], 0:8, :]
-            hit = codes[0:1, :] == target
-            for k in range(1, top_k):
-                hit = jnp.logical_or(hit, codes[k : k + 1, :] == target)
-            one_hot = jnp.where(hit, 1.0, 0.0).astype(BF16)
-            picked = jnp.dot(one_hot, tok[srcs[i]], preferred_element_type=F32).astype(BF16)
-            xe[slot, 0, i * capacity : (i + 1) * capacity, :] = picked[:capacity]
-            xe[slot, 1, i * capacity : (i + 1) * capacity, :] = picked[capacity:]
+            one_hot = one_hot_rows(meta[srcs[i], 0:8, :], target)
+            for quarter in quarters:
+                cols = columns(quarter)
+                whole = pick([int(is_whole(quarter, unit[i // 2])) for unit in units], u)
+
+                @pl.when(whole == 1)
+                def _(i=i, cols=cols, one_hot=one_hot):
+                    picked = jnp.dot(one_hot, tok[srcs[i], :, cols], preferred_element_type=F32).astype(BF16)
+                    xe[slot, 0, i * capacity : (i + 1) * capacity, cols] = picked[:capacity]
+                    xe[slot, 1, i * capacity : (i + 1) * capacity, cols] = picked[capacity:]
+
+                @pl.when(whole == 0)
+                def _(i=i, cols=cols):
+                    xe[slot, 0, i * capacity : (i + 1) * capacity, cols] = tok[srcs[i], 0:capacity, cols]
+                    xe[slot, 1, i * capacity : (i + 1) * capacity, cols] = tok[srcs[i], capacity:pair, cols]
 
         @pl.when(u >= 1)
         def _():
@@ -415,20 +450,22 @@
         return 0
 
     lax.fori_loop(0, 8, combine, 0)
+    n_whole = sum(whole for whole, _ in slots)
+    await_sent(link_send.at[0], tok.at[pl.ds(0, n_whole)])
+    for group in range(5):
+        await_picks_sent(group)
+    await_sent(chip_send.at[0], tok.at[pl.ds(0, n_whole + 1)])
+    await_sent(meta_send.at[0], meta.at[pl.ds(0, 2 * len(slots) + 1)])
     await_bytes(hop2_recv.at[0], hop2)
     for h in range(2):
-        y_out[:, h * half_cols : (h + 1) * half_cols] = (base[h] + (hop2[h, 0] + hop2[h, 1])).astype(BF16)
-
-    def await_sent(sem, ref):
-        rdma(ref, ref, sem, sem, partner).wait_send()
-
-    await_sent(link_send.at[0], tok.at[pl.ds(0, n_steps)])
-    await_sent(chip_send.at[0], tok.at[pl.ds(0, n_steps + 1)])
-    await_sent(meta_send.at[0], meta.at[pl.ds(0, 2 * n_steps + 1)])
+        tok[me, :, h * half_cols : (h + 1) * half_cols] = (base[h] + (hop2[h, 0] + hop2[h, 1])).astype(BF16)
+    result = pltpu.make_async_copy(tok.at[me], y_out, load_sem.at[0])
+    result.start()
     await_sent(direct_send.at[0], r_buf.at[:, pl.ds(0, 20)])
     await_sent(relay_send.at[0], r_buf.at[:, pl.ds(0, 16)])
     await_sent(hop1_send.at[0], hop1)
     await_sent(hop2_send.at[0], hop2)
+    result.wait()
 
 
 def solution(mesh):
@@ -456,9 +493,10 @@
                        jax.ShapeDtypeStruct((2, num_ep, pair, half), BF16),
                        jax.ShapeDtypeStruct((4, 2, 2, pair, half), BF16)),
             in_specs=[anywhere] + [vmem] * 3 + [anywhere] * 3 + [vmem] + [anywhere] * 3,
-            out_specs=(vmem, anywhere, anywhere),
+            out_specs=(anywhere, anywhere, anywhere),
             scratch_shapes=[
                 pltpu.VMEM((num_ep, tok_count, hidden), BF16),
+                pltpu.VMEM((5, 4, 2 * pair, hidden // 4), BF16),
                 pltpu.VMEM((num_ep, 16, tok_count), F32),
                 pltpu.VMEM((2, tok_count, half), F32),
                 pltpu.VMEM((local_experts, hidden, ff), BF16),
@@ -470,7 +508,7 @@
                 pltpu.VMEM((2, 3, tok_count, half), F32),
                 pltpu.VMEM((2, 2, tok_count // 2, half), F32),
                 pltpu.VMEM((2, 2, tok_count, half), F32),
-                dma((4,)), dma((1,)), dma((1,)), dma((1,)), dma((15,)), dma((16,)), dma((15,)), dma((16,)), dma((2,)),
+                dma((4,)), dma((1,)), dma((5,)), dma((1,)), dma((1,)), dma((15,)), dma((16,)), dma((15,)), dma((16,)), dma((2,)),
                 dma((1,)), dma((1,)), dma((2, 4)), dma((4,)), dma((1,)), dma((1,)), dma((1,)), dma((1,)),
             ],
             compiler_params=pltpu.CompilerParams(collective_id=0, has_side_effects=True, vmem_limit_bytes=VMEM_LIMIT),

time: 156 us -> 148 us (0.949)
  Pallas kernels: 154 us -> 146 us
    pallas_call x1, Pallas kernels: 154 us -> 146 us  [device_step(): pl.pallas_call(functools.partial(layer_kernel, side, capacity), out_shape...]
where the time goes in v4:
time: 148 us
  Pallas kernels  146 us (99%)
  local copies, waits for them, and re-layouts  2.06 us (1%)
    pallas_call x1, Pallas kernels, device_step(): pl.pallas_call(functools.partial(layer_kernel, side, capacity), out_shape...  146 us

profile of v4, /device:TPU:97, one launch (start us, length us, event | category | flops | bytes accessed | tf_op | source)
XLA Modules:
  0.0 148.2 jit_solution(12655095083319499271)
XLA Ops:
  0.0 146.1 %moe_layer.1 = (bf16[256,1536]{1,0:T(8,128)(2,1)}, bf16[2,32,96,768]{3,2,1,0:T(8,128)(2,1)}, bf16[4,2,2,96,768]{4,3,2,1,0:T(8,128)(2,1)}) custom-call(bf16[256,1536]{1,0:T(8,128)(2,1)} %tok_in.1, s32[6,256]{1,0:T(8,128)} %bitcast.3, s32[6,256]{1,0:T(8,128)} %bitcast.4, f32[6,256]{1,0:T(8,128)} %bitcast.5, bf16[1536,1024]{1,0:T(8,128)(2,1)} %sw1_in.1, ...), custom_call_target="tpu_custom_call" | custom-call | tf_op jit(solution)/shard_map/moe_layer/pallas_call | solution.py:490
  146.1 2.1 %copy.13 = bf16[256,1536]{1,0:T(8,128)(2,1)} copy(bf16[256,1536]{1,0:T(8,128)(2,1)} %get-tuple-element.6) | data formatting | bytes 1572864

commit v5 on v4

--- a/solution.py
+++ b/solution.py
@@ -25,21 +25,43 @@
     return tuple(moved)
 
 
+TREE = (((1, 0), (0, 0)), ((0, 1), (0, 0)), ((2, 0), (1, 0)), ((0, 2), (0, 1)), ((2, 3), (2, 0)),
+        ((0, 3), (0, 0)), ((3, 0), (0, 0)), ((3, 1), (0, 1)), ((1, 1), (0, 1)), ((3, 3), (2, 3)),
+        ((1, 3), (1, 0)), ((2, 2), (2, 3)), ((1, 2), (0, 2)), ((2, 1), (2, 0)), ((3, 2), (0, 2)))
+SLOT = {chip: i for i, (chip, _) in enumerate(TREE)}
+INNER = {parent for _, parent in TREE}
+
+
+def turn(chip, times):
+    for _ in range(times % 4):
+        chip = (-chip[1] % 4, chip[0])
+    return chip
+
+
+def node(quarter, at):
+    return turn((-at[0] % 4, -at[1] % 4), 4 - quarter)
+
+
+def is_whole(quarter, at):
+    return node(quarter, at) in INNER
+
+
+def carries_meta(quarter, at):
+    return quarter == min(range(4), key=lambda k: (SLOT[node(k, at)], k))
+
+
 def plan_gather():
+    ways = [((way, 0) if axis == 0 else (0, way)) for axis, way in DIRS]
     slots = []
-    for kind, g in (('F1w', 0), ('F1a', 0), ('F2', 0), ('Ga', 0), ('F1f', 0), ('F2', -1), ('F2', 1), ('F2', 2), ('Ga', -1),
-                    ('Ga', 1), ('Ga', 2), ('Gb', 0), ('Gb', -1), ('Gb', 1), ('Gb', 2)):
+    for chip, parent in TREE:
+        step = ((chip[0] - parent[0]) % 4, (chip[1] - parent[1]) % 4)
         messages = []
-        for d, (a, v) in enumerate(DIRS):
-            at = [0, 0]
-            quarter = (a, v) if kind in ('F1w', 'F1f') else (a, -v) if kind == 'F1a' else (1 - a, -v if kind == 'Ga' else v)
-            if kind in ('F1f', 'Gb'):
-                at[a] = -v
-            if kind in ('F2', 'Ga', 'Gb'):
-                at[1 - a] = wrap(g * quarter[1])
-            messages.append((d, quarter, tuple(at)))
-        slots.append((kind[0] == 'F', messages))
-    sends = {-1: (0, 1, 2, 3), 0: (4, 5), 1: (6,), 4: (7, 8, 9), 5: (10, 11), 9: (12, 13), 10: (14,)}
+        for d, way in enumerate(ways):
+            quarter = next(k for k in range(4) if turn(step, k) == (way[0] % 4, way[1] % 4))
+            at = turn(parent, quarter)
+            messages.append((d, quarter, (wrap(-at[0]), wrap(-at[1]))))
+        slots.append((chip in INNER, messages))
+    sends = {-1: (0, 1), 0: (2,), 1: (3,), 2: (4, 5, 6, 7, 8), 4: (9,), 5: (10,), 6: (11,), 7: (12,), 8: (13,), 9: (14,)}
     return slots, sends
 
 
@@ -53,20 +75,6 @@
     return units, [max(done[at] for at in unit) for unit in units]
 
 
-def is_whole(quarter, at):
-    h, w = quarter
-    return at[1 - h] in (0, -w)
-
-
-def carries_meta(quarter, at):
-    h, w = quarter
-    if w != 1 or at[h] == 0:
-        return False
-    if at[1 - h] == 0:
-        return True
-    return h == (1 if abs(at[0]) == 1 and at[1] == 2 else 0)
-
-
 def place(side):
     me = lax.axis_index('ep')
     chip = me // 2
@@ -92,7 +100,7 @@
     me, x, y, c = place(side)
     slots, sends = plan_gather()
     units, ready = plan_units(slots)
-    quarters = [(h, w) for h in range(2) for w in (1, -1)]
+    quarters = range(4)
     top_k = ids_ref.shape[0]
     n_tok, hidden = tok_in.shape
     half_cols, half_rows = hidden // 2, n_tok // 2
@@ -144,7 +152,7 @@
     pl.semaphore_wait(barrier, 9)
 
     def columns(quarter):
-        return pl.ds(quarters.index(quarter) * quarter_cols, quarter_cols)
+        return pl.ds(quarter * quarter_cols, quarter_cols)
 
     def view(quarter, src):
         return tok.at[src, :, columns(quarter)]
@@ -312,6 +320,8 @@
         pltpu.make_async_copy(r_buf.at[0, pl.ds(0, 2 * side)], rows.at[0, 0], out_sem.at[slot]).wait()
 
     n_units = len(units)
+    n_early = 1 + max(k for k, unit in enumerate(units) for at in unit if max(at) < 2)
+    assert n_early < n_units and max(sends) < ready[n_early - 1]
 
     def do_unit(u, _):
         done = 0
@@ -321,6 +331,10 @@
 
             @pl.when(u == k)
             def _(lo=lo, hi=hi, k=k):
+                if k == n_early:
+                    await_out((k - 1) % 2)
+                    send_direct(1)
+                    send_direct(2)
                 for i in range(lo, hi):
                     do_slot(i)
                 for i in range(lo + 1 if lo else 0, hi + 1):
@@ -345,14 +359,9 @@
                     xe[slot, 0, i * capacity : (i + 1) * capacity, cols] = tok[srcs[i], 0:capacity, cols]
                     xe[slot, 1, i * capacity : (i + 1) * capacity, cols] = tok[srcs[i], capacity:pair, cols]
 
-        @pl.when(u >= 1)
+        @pl.when(jnp.logical_and(u >= 1, u != n_early))
         def _():
             await_out(1 - slot)
-
-        @pl.when(u == n_units - 3)
-        def _():
-            send_direct(1)
-            send_direct(2)
 
         def do_expert(j, _):
             a = jnp.dot(xe[slot, j], w1[j], preferred_element_type=F32)

time: 148 us -> 145 us (0.980)
  Pallas kernels: 146 us -> 143 us
    pallas_call x1, Pallas kernels: 146 us -> 143 us  [device_step(): pl.pallas_call(functools.partial(layer_kernel, side, capacity), out_shape...]
where the time goes in v5:
time: 145 us
  Pallas kernels  143 us (99%)
  local copies, waits for them, and re-layouts  2.06 us (1%)
    pallas_call x1, Pallas kernels, device_step(): pl.pallas_call(functools.partial(layer_kernel, side, capacity), out_shape...  143 us

profile of v5, /device:TPU:97, one launch (start us, length us, event | category | flops | bytes accessed | tf_op | source)
XLA Modules:
  0.0 145.2 jit_solution(16205846852590577687)
XLA Ops:
  0.0 143.1 %moe_layer.1 = (bf16[256,1536]{1,0:T(8,128)(2,1)}, bf16[2,32,96,768]{3,2,1,0:T(8,128)(2,1)}, bf16[4,2,2,96,768]{4,3,2,1,0:T(8,128)(2,1)}) custom-call(bf16[256,1536]{1,0:T(8,128)(2,1)} %tok_in.1, s32[6,256]{1,0:T(8,128)} %bitcast.3, s32[6,256]{1,0:T(8,128)} %bitcast.4, f32[6,256]{1,0:T(8,128)} %bitcast.5, bf16[1536,1024]{1,0:T(8,128)(2,1)} %sw1_in.1, ...), custom_call_target="tpu_custom_call" | custom-call | tf_op jit(solution)/shard_map/moe_layer/pallas_call | solution.py:499
  143.1 2.1 %copy.13 = bf16[256,1536]{1,0:T(8,128)(2,1)} copy(bf16[256,1536]{1,0:T(8,128)(2,1)} %get-tuple-element.6) | data formatting | bytes 1572864

commit v6 on v5

--- a/solution.py
+++ b/solution.py
@@ -92,16 +92,16 @@
     return (jax.nn.silu(a) * b).astype(BF16)
 
 
-def layer_kernel(side, capacity, tok_in, ids_ref, slots_ref, gates_ref, sw1_in, sw3_in, sw2_in, sg_ref, w1_in, w3_in, w2_in,
+def layer_kernel(side, capacity, tok_in, ids_in, slots_in, gates_in, sw1_in, sw3_in, sw2_in, sg_in, w1_in, w3_in, w2_in,
                  y_out, r_buf, relay,
-                 tok, picked_rows, meta, base, w1, w3, w2, xe, rows, wt, part, hop1, hop2,
-                 load_sem, link_send, pick_send, chip_send, meta_send, link_recv, chip_recv, meta_link_recv, meta_chip_recv, out_sem,
+                 ids_ref, slots_ref, gates_ref, sg_ref, tok, picked_rows, meta, gates, base, w1, w3, w2, xe, rows, wt, part, hop1, hop2,
+                 load_sem, link_send, pick_send, chip_send, meta_send, link_recv, chip_recv, meta_link_recv, meta_chip_recv, gates_send, gates_recv, out_sem,
                  direct_send, relay_send, rows_recv, relay_recv, hop1_send, hop1_recv, hop2_send, hop2_recv):
     me, x, y, c = place(side)
     slots, sends = plan_gather()
     units, ready = plan_units(slots)
     quarters = range(4)
-    top_k = ids_ref.shape[0]
+    top_k = ids_in.shape[0]
     n_tok, hidden = tok_in.shape
     half_cols, half_rows = hidden // 2, n_tok // 2
     quarter_cols = hidden // 4
@@ -127,8 +127,14 @@
 
     partner = me + 1 - 2 * c
 
+    barrier = pltpu.get_barrier_semaphore()
+    for to in [neighbour(d, core) for d in range(4) for core in range(2)] + [partner]:
+        pl.semaphore_signal(barrier, inc=1, device_id={'ep': to}, device_id_type=MESH)
     tok_load = pltpu.make_async_copy(tok_in, tok.at[me], load_sem.at[0])
-    tok_load.start()
+    small_loads = [pltpu.make_async_copy(src, dst, load_sem.at[4 + k]) for k, (src, dst) in enumerate(
+        ((ids_in, ids_ref), (slots_in, slots_ref), (gates_in, gates_ref), (sg_in, sg_ref)))]
+    for load in [tok_load] + small_loads:
+        load.start()
     shared_loads, expert_loads = [], []
     for j in range(2):
         cols = pl.ds(j * ff, ff)
@@ -140,14 +146,13 @@
     for load in shared_loads:
         load.start()
 
-    barrier = pltpu.get_barrier_semaphore()
-    for to in [neighbour(d, core) for d in range(4) for core in range(2)] + [partner]:
-        pl.semaphore_signal(barrier, inc=1, device_id={'ep': to}, device_id_type=MESH)
+    for load in small_loads:
+        load.wait()
     slot_of = slots_ref[...]
     meta[me, 0:top_k, :] = jnp.where(slot_of >= 0, ids_ref[...] * capacity + slot_of, -1).astype(F32)
-    meta[me, 8 : 8 + top_k, :] = gates_ref[...]
     meta[me, top_k:8, :] = jnp.full((8 - top_k, n_tok), -1.0, F32)
-    meta[me, 8 + top_k : 16, :] = jnp.zeros((8 - top_k, n_tok), F32)
+    gates[me, 0:top_k, :] = gates_ref[...]
+    gates[me, top_k:8, :] = jnp.zeros((8 - top_k, n_tok), F32)
     tok_load.wait()
     pl.semaphore_wait(barrier, 9)
 
@@ -192,9 +197,13 @@
                 for core in range(2):
                     rdma(picked_rows.at[group_of[i], d, pl.ds(core * pair, pair)],
                          tok.at[src, pl.ds(0, pair), columns(quarter)], pick_send.at[group_of[i]], link_recv.at[i], neighbour(d, core)).start()
-            if carries_meta(quarter, shift(*DIRS[d], at)):
+            to_at = shift(*DIRS[d], at)
+            if carries_meta(quarter, to_at):
                 for core in (None,) if whole else (0, 1):
                     rdma(meta.at[src], meta.at[src], meta_send.at[0], meta_link_recv.at[i], neighbour(d, core)).start()
+                if 0 in to_at:
+                    assert whole
+                    rdma(gates.at[src], gates.at[src], gates_send.at[0], gates_recv.at[i], neighbour(d)).start()
 
     def await_bytes(sem, ref):
         rdma(ref, ref, sem, sem, partner).wait_recv()
@@ -207,6 +216,10 @@
         await_bytes(link_recv.at[i], tok.at[0] if whole else tok.at[0, pl.ds(0, 2 * pair)])
         if metas(i):
             await_bytes(meta_link_recv.at[i], meta.at[pl.ds(0, metas(i) * (1 if whole else 2))])
+        arrived = [(quarter, shift(*DIRS[d], at)) for d, quarter, at in messages]
+        in_line = sum(carries_meta(quarter, at) and 0 in at for quarter, at in arrived)
+        if in_line:
+            await_bytes(gates_recv.at[i], gates.at[pl.ds(0, in_line)])
 
     def do_slot(i):
         await_slot(i)
@@ -414,15 +427,15 @@
         bx, by = lax.rem(x + jnp.where(h == 0, 0, b), side), lax.rem(y + jnp.where(h == 0, b, 0), side)
         dest = (by * side + bx) * 2 + c
         codes = meta[dest, 0:8, :]
-        gates = meta[dest, 8:16, :]
+        shares = gates[dest]
 
         def weights(g, _):
             gx, gy = jnp.where(h == 0, g // 2, x), jnp.where(h == 0, y, g // 2)
             source = (gy * side + gx) * 2 + lax.rem(g, 2)
             goal = (row_ids + source * pair).astype(F32)
-            w = jnp.where(codes[0:1, :] == goal, gates[0:1, :], 0.0)
+            w = jnp.where(codes[0:1, :] == goal, shares[0:1, :], 0.0)
             for k in range(1, top_k):
-                w = jnp.where(codes[k : k + 1, :] == goal, gates[k : k + 1, :], w)
+                w = jnp.where(codes[k : k + 1, :] == goal, shares[k : k + 1, :], w)
             at = pl.ds(pl.multiple_of(g * pair, pair), pair)
             hi = w.astype(BF16)
             w = w - hi.astype(F32)
@@ -465,16 +478,22 @@
         await_picks_sent(group)
     await_sent(chip_send.at[0], tok.at[pl.ds(0, n_whole + 1)])
     await_sent(meta_send.at[0], meta.at[pl.ds(0, 2 * len(slots) + 1)])
+    await_sent(gates_send.at[0], gates.at[pl.ds(0, 2 * (side - 1))])
     await_bytes(hop2_recv.at[0], hop2)
-    for h in range(2):
-        tok[me, :, h * half_cols : (h + 1) * half_cols] = (base[h] + (hop2[h, 0] + hop2[h, 1])).astype(BF16)
-    result = pltpu.make_async_copy(tok.at[me], y_out, load_sem.at[0])
-    result.start()
+    results = []
+    for p in range(2):
+        piece = pl.ds(p * half_rows, half_rows)
+        for h in range(2):
+            total = base[h, piece] + (hop2[h, 0, piece] + hop2[h, 1, piece])
+            tok[me, piece, h * half_cols : (h + 1) * half_cols] = total.astype(BF16)
+        results.append(pltpu.make_async_copy(tok.at[me, piece], y_out.at[piece], load_sem.at[p]))
+        results[-1].start()
     await_sent(direct_send.at[0], r_buf.at[:, pl.ds(0, 20)])
     await_sent(relay_send.at[0], r_buf.at[:, pl.ds(0, 16)])
     await_sent(hop1_send.at[0], hop1)
     await_sent(hop2_send.at[0], hop2)
-    result.wait()
+    for result in results:
+        result.wait()
 
 
 def solution(mesh):
@@ -484,7 +503,7 @@
     row_spec = P(('dp', 'ep'), None)
     replicated = P()
     expert_spec = P('ep', None, None)
-    vmem, anywhere = pl.BlockSpec(memory_space=pltpu.VMEM), pl.BlockSpec(memory_space=pl.ANY)
+    anywhere = pl.BlockSpec(memory_space=pl.ANY)
     dma = pltpu.SemaphoreType.DMA
 
     def device_step(tokens, expert_ids, gate_vals, slots, shared_w1, shared_w3, shared_w2, shared_gate, expert_w1, expert_w3, expert_w2):
@@ -501,12 +520,17 @@
             out_shape=(jax.ShapeDtypeStruct((tok_count, hidden), BF16),
                        jax.ShapeDtypeStruct((2, num_ep, pair, half), BF16),
                        jax.ShapeDtypeStruct((4, 2, 2, pair, half), BF16)),
-            in_specs=[anywhere] + [vmem] * 3 + [anywhere] * 3 + [vmem] + [anywhere] * 3,
+            in_specs=[anywhere] * 11,
             out_specs=(anywhere, anywhere, anywhere),
             scratch_shapes=[
+                pltpu.VMEM((top_k, tok_count), jnp.int32),
+                pltpu.VMEM((top_k, tok_count), jnp.int32),
+                pltpu.VMEM((top_k, tok_count), F32),
+                pltpu.VMEM((hidden,), BF16),
                 pltpu.VMEM((num_ep, tok_count, hidden), BF16),
                 pltpu.VMEM((5, 4, 2 * pair, hidden // 4), BF16),
-                pltpu.VMEM((num_ep, 16, tok_count), F32),
+                pltpu.VMEM((num_ep, 8, tok_count), F32),
+                pltpu.VMEM((num_ep, 8, tok_count), F32),
                 pltpu.VMEM((2, tok_count, half), F32),
                 pltpu.VMEM((local_experts, hidden, ff), BF16),
                 pltpu.VMEM((local_experts, hidden, ff), BF16),
@@ -517,7 +541,7 @@
                 pltpu.VMEM((2, 3, tok_count, half), F32),
                 pltpu.VMEM((2, 2, tok_count // 2, half), F32),
                 pltpu.VMEM((2, 2, tok_count, half), F32),
-                dma((4,)), dma((1,)), dma((5,)), dma((1,)), dma((1,)), dma((15,)), dma((16,)), dma((15,)), dma((16,)), dma((2,)),
+                dma((8,)), dma((1,)), dma((5,)), dma((1,)), dma((1,)), dma((15,)), dma((6,)), dma((15,)), dma((6,)), dma((1,)), dma((3,)), dma((2,)),
                 dma((1,)), dma((1,)), dma((2, 4)), dma((4,)), dma((1,)), dma((1,)), dma((1,)), dma((1,)),
             ],
             compiler_params=pltpu.CompilerParams(collective_id=0, has_side_effects=True, vmem_limit_bytes=VMEM_LIMIT),

time: 145 us -> 144 us (level)
  no operation moved by 1% of the time
where the time goes in v6:
time: 144 us
  Pallas kernels  142 us (99%)
  local copies, waits for them, and re-layouts  2.06 us (1%)
    pallas_call x1, Pallas kernels, device_step(): pl.pallas_call(functools.partial(layer_kernel, side, capacity), out_shape...  142 us

profile of v6, /device:TPU:97, one launch (start us, length us, event | category | flops | bytes accessed | tf_op | source)
XLA Modules:
  0.0 143.9 jit_solution(10369166336921730545)
XLA Ops:
  0.0 141.8 %moe_layer.1 = (bf16[256,1536]{1,0:T(8,128)(2,1)}, bf16[2,32,96,768]{3,2,1,0:T(8,128)(2,1)}, bf16[4,2,2,96,768]{4,3,2,1,0:T(8,128)(2,1)}) custom-call(bf16[256,1536]{1,0:T(8,128)(2,1)} %tok_in.1, s32[6,256]{1,0:T(8,128)} %bitcast.3, s32[6,256]{1,0:T(8,128)} %bitcast.4, f32[6,256]{1,0:T(8,128)} %bitcast.5, bf16[1536,1024]{1,0:T(8,128)(2,1)} %sw1_in.1, ...), custom_call_target="tpu_custom_call" | custom-call | tf_op jit(solution)/shard_map/moe_layer/pallas_call | solution.py:518
  141.8 2.1 %copy.13 = bf16[256,1536]{1,0:T(8,128)(2,1)} copy(bf16[256,1536]{1,0:T(8,128)(2,1)} %get-tuple-element.6) | data formatting | bytes 1572864

commit v7 on v6

--- a/solution.py
+++ b/solution.py
@@ -408,9 +408,12 @@
         def _():
             send_direct(3)
 
+        @pl.when(n == 5)
+        def _():
+            forward(3)
+
         @pl.when(n == 6)
         def _():
-            forward(3)
             await_bytes(hop1_recv.at[0], hop1)
             for hh in range(2):
                 for w in range(2):

time: 144 us -> 144 us (level)
  no operation moved by 1% of the time
where the time goes in v7:
time: 144 us
  Pallas kernels  142 us (99%)
  local copies, waits for them, and re-layouts  2.06 us (1%)
    pallas_call x1, Pallas kernels, device_step(): pl.pallas_call(functools.partial(layer_kernel, side, capacity), out_shape...  142 us

profile of v7, /device:TPU:97, one launch (start us, length us, event | category | flops | bytes accessed | tf_op | source)
XLA Modules:
  0.0 143.9 jit_solution(16641805143396127272)
XLA Ops:
  0.0 141.8 %moe_layer.1 = (bf16[256,1536]{1,0:T(8,128)(2,1)}, bf16[2,32,96,768]{3,2,1,0:T(8,128)(2,1)}, bf16[4,2,2,96,768]{4,3,2,1,0:T(8,128)(2,1)}) custom-call(bf16[256,1536]{1,0:T(8,128)(2,1)} %tok_in.1, s32[6,256]{1,0:T(8,128)} %bitcast.3, s32[6,256]{1,0:T(8,128)} %bitcast.4, f32[6,256]{1,0:T(8,128)} %bitcast.5, bf16[1536,1024]{1,0:T(8,128)(2,1)} %sw1_in.1, ...), custom_call_target="tpu_custom_call" | custom-call | tf_op jit(solution)/shard_map/moe_layer/pallas_call | solution.py:521
  141.8 2.1 %copy.13 = bf16[256,1536]{1,0:T(8,128)(2,1)} copy(bf16[256,1536]{1,0:T(8,128)(2,1)} %get-tuple-element.6) | data formatting | bytes 1572864
